TPU v7x, 32 devices: a whole 2x2x4 slice. The times are simulated.
32 devices in a mesh: din: 4 (over x, core), dout: 8 (over z, y).
Axes of the slice: x: 2, y: 2, z: 4, core: 2. Of those that a mesh axis runs over, the one named last changes fastest.
Arguments:
- inputs: float32 [16, 8192], P('dout', 'din'), may hold values from -1.5 to 1.5
- out_grad: float32 [16, 28672], P('din', 'dout'), may hold values from -6 to 6
- weight: float32 [8192, 28672], P('din', 'dout'), may hold values from -0.03125 to 0.03125
Outputs:
- input_grad: float32 [16, 8192], P('dout', 'din')
- weight_grad: float32 [8192, 28672], P('din', 'dout')
All inputs are finite; a program needn't handle non-finite values.
Results may differ from a plain program's by a relative error of at most 0.000071.
Values sent between devices are 32-bit elements; how exact they have to be, the bound alone decides.
No kernel may reach another device: no remote copies, remote signals or barrier semaphores. Data moves between devices by JAX's collectives and lax.ppermute only.
A program may use at most 128 MiB of HBM per device.

v0:
```python
import jax
import jax.numpy as jnp
from jax import lax
from jax.sharding import PartitionSpec as P


def contract_rows(left, right):
    return lax.dot_general(
        left,
        right,
        (((0,), (0,)), ((), ())),
        precision=lax.Precision.HIGHEST,
        preferred_element_type=jnp.float32,
    )


def contract_units(left, right):
    return lax.dot_general(
        left,
        right,
        (((1,), (1,)), ((), ())),
        precision=lax.Precision.HIGHEST,
        preferred_element_type=jnp.float32,
    )


def body(inputs, out_grad, weight):
    gradients = lax.all_gather(out_grad, "din", axis=0, tiled=True)
    weight_grad = contract_rows(lax.all_gather(inputs, "dout", axis=0, tiled=True), gradients)
    input_grad = lax.psum_scatter(
        contract_units(gradients, weight), "dout", scatter_dimension=0, tiled=True
    )
    return (input_grad, weight_grad)


def solution(mesh):
    placed = (P("dout", "din"), P("din", "dout"), P("din", "dout"))
    return jax.shard_map(
        body,
        mesh=mesh,
        in_specs=placed,
        out_specs=(P("dout", "din"), P("din", "dout")),
        check_vma=False,
    )
```

profile of v0, /device:TPU:0, one launch (start us, length us, event | category | flops | bytes accessed | tf_op | source)
XLA Modules:
  0.0 124.4 jit_solution(11529499844994896099)
XLA Ops:
  7.2 0.0 copy-start
  7.2 0.0 all-reduce.3.cloned.1.call-start
  7.2 7.3 %all-gather = f32[4,4,3584]{2,1,0:T(4,128)S(1)} all-gather(f32[1,4,3584]{2,1,0:T(4,128)} %bitcast.7), channel_id=1, replica_groups=mesh['din'=4,'dout'=8] {'din'}, dimensions={0}, use_global_device_ids=true | all-gather | bytes 286720 | tf_op jit(solution)/shard_map/all_gather | solution.py:28
  14.5 0.1 reshape.5
  14.6 0.0 copy-start.1
  14.6 29.5 %fusion = f32[16,2048]{1,0:T(8,128)} fusion(f32[16,3584]{1,0:T(8,128)S(1)} %reshape.5, f32[2048,3584]{1,0:T(8,128)} %param.5), kind=kOutput, calls=%fused_computation.1 | convolution fusion | flops 1409286144 | bytes 29720576 | tf_op jit(solution)/shard_map/dot_general | solution.py:18
  44.1 0.0 all-reduce.3.cloned.1.call-update
  44.1 0.0 copy-done
  44.1 31.2 %all-gather.1 = f32[8,2,2048]{2,1,0:T(2,128)S(1)} all-gather(f32[1,2,2048]{2,1,0:T(2,128)S(1)} %bitcast.8), channel_id=1, replica_groups=mesh['din'=4,'dout'=8] {'dout'}, dimensions={0}, use_global_device_ids=true | all-gather | bytes 147456 | tf_op jit(solution)/shard_map/all_gather | solution.py:29
  75.3 0.1 reshape.7
  75.4 26.7 %fusion.1 = f32[2048,3584]{1,0:T(8,128)} fusion(f32[16,2048]{1,0:T(8,128)S(1)} %reshape.7, f32[16,3584]{1,0:T(8,128)S(1)} %reshape.5), kind=kOutput, calls=%fused_computation.2 | convolution fusion | flops 1409286144 | bytes 29720576 | tf_op jit(solution)/shard_map/dot_general | solution.py:8
  102.2 0.0 copy-done.1
  102.2 0.6 dynamic-slice
  103.4 12.7 %all-reduce.3.cloned.1.call-done = f32[16,2048]{1,0:T(8,128)} async-done(((f32[16,2048]{1,0:T(8,128)}), f32[16,2048]{1,0:T(8,128)}) %all-reduce.3.cloned.1.call-update) | async-done | bytes 131088
  116.1 1.5 %constant_dynamic-slice_fusion = f32[2,2048]{1,0:T(2,128)} fusion(f32[16,2048]{1,0:T(8,128)} %all-reduce.3.cloned.1.call-done, u32[]{:T(128)S(6)} %multiply.1), kind=kLoop, calls=%fused_computation | loop fusion | bytes 32772
Async XLA Ops:
  7.2 37.0 %copy-start = (f32[2,2048]{1,0:T(2,128)S(1)}, f32[2,2048]{1,0:T(2,128)}, u32[]{:S(2)}) copy-start(f32[2,2048]{1,0:T(2,128)} %param.3) | copy-start | bytes 49156
  7.2 108.9 %all-reduce.3.cloned.1.call-start = ((), (), s32[]{:S(2)}) async-start(), calls=%async_computation | async-start | bytes 262144
  14.6 87.6 %copy-start.1 = (u32[32]{0:T(128)S(1)}, u32[32]{0:T(128)}, u32[]{:S(2)}) copy-start(u32[32]{0:T(128)} %constant.3) | copy-start | bytes 388
Sparse Core Ops, SparseCore 0:
  44.2 71.7 all-reduce.2
where the time goes:
time: 125 us; the launch traced here: 124 us
  matrix products  56.2 us (45%)
  blocking collectives  38.5 us (31%)
  between operations  14.7 us (12%)
  waiting for transfers between devices  12.7 us (10%)
  local copies, waits for them, and re-layouts  2.22 us (2%)
    all_gather x1, blocking collectives, body(): lax.all_gather(inputs, 'dout', axis=0, tiled=True)  31.2 us
    dot_general x1, matrix products, contract_units(): lax.dot_general(left, right, (((1,), (1,)), ((), ())), precision=lax.Prec...  29.5 us
    dot_general x1, matrix products, contract_rows(): lax.dot_general(left, right, (((0,), (0,)), ((), ())), precision=lax.Prec...  26.7 us
    unnamed x2, waiting for transfers between devices  12.7 us
    all_gather x1, blocking collectives, body(): gradients = lax.all_gather(out_grad, 'din', axis=0, tiled=True)  7.26 us
  transfers between devices with their start and end apart: 1, of which 1 were waited for; matrix products, arithmetic and copies ran while one was open for 22% of the time, Pallas kernels for 0%

commit v1 on v0

v1 whole, which is shorter than its diff:
```python
import functools

import jax
import jax.numpy as jnp
from jax import lax
from jax.experimental import pallas as pl
from jax.experimental.pallas import tpu as pltpu
from jax.sharding import PartitionSpec as P


F32 = jnp.float32
BF16 = jnp.bfloat16
TN = (((0,), (0,)), ((), ()))
NT = (((1,), (1,)), ((), ()))

UNITS_TILE = 256
BOTH_TILE = 128
OUTER_TILE = 128
READ_SLOTS = 4
WRITE_SLOTS = 3


def plain_body(inputs, out_grad, weight):
    gradients = lax.all_gather(out_grad, "din", axis=0, tiled=True)
    rows = lax.all_gather(inputs, "dout", axis=0, tiled=True)
    weight_grad = lax.dot_general(
        rows, gradients, TN, precision=lax.Precision.HIGHEST, preferred_element_type=F32
    )
    partial = lax.dot_general(
        gradients, weight, NT, precision=lax.Precision.HIGHEST, preferred_element_type=F32
    )
    input_grad = lax.psum_scatter(partial, "dout", scatter_dimension=0, tiled=True)
    return (input_grad, weight_grad)


def halves(value):
    high = value.astype(BF16)
    low = (value - high.astype(F32)).astype(BF16)
    return high, low


def swap(value, axis, size, distance):
    return lax.ppermute(value, axis, [(i, i ^ distance) for i in range(size)])


def in_order(pieces, me):
    count = len(pieces)
    ordered = []
    for position in range(count):
        value = pieces[0][...]
        for s in range(1, count):
            value = jnp.where((me ^ s) == position, pieces[s][...], value)
        ordered.append(value)
    return ordered


def multiply(split_ref, rows, value):
    high, low = halves(value)
    both = lax.dot_general(split_ref[: 2 * rows], high, NT, preferred_element_type=F32)
    rest = lax.dot_general(split_ref[:rows], low, NT, preferred_element_type=F32)
    return both[:rows] + both[rows:] + rest


def aligned(index, tile):
    return pl.ds(pl.multiple_of(index * tile, tile), tile)


class Reader:
    def __init__(self, w_ref, slots, sems, first, steps):
        self.w, self.slots, self.sems = w_ref, slots, sems
        self.first, self.steps = first, steps
        self.ahead = min(slots.shape[0] - 1, steps)

    def copy(self, step):
        count, tile = self.slots.shape[:2]
        slot = lax.rem(step, count)
        return pltpu.make_async_copy(
            self.w.at[aligned(self.first + step, tile), :],
            self.slots.at[slot],
            self.sems.at[slot],
        )

    def begin(self):
        for step in range(self.ahead):
            self.copy(step).start()

    def take(self, step):
        self.copy(step).wait()

        @pl.when(step + self.ahead < self.steps)
        def _():
            self.copy(step + self.ahead).start()

        return self.slots[lax.rem(step, self.slots.shape[0])]


class Writer:
    def __init__(self, left_ref, split_ref, out_ref, slots, sems, first, steps):
        self.left, self.split, self.out = left_ref, split_ref, out_ref
        self.slots, self.sems = slots, sems
        self.first, self.steps = first, steps

    def copy(self, step):
        count, tile = self.slots.shape[:2]
        slot = lax.rem(step, count)
        return pltpu.make_async_copy(
            self.slots.at[slot],
            self.out.at[aligned(self.first + step, tile), :],
            self.sems.at[slot],
        )

    def make(self, step):
        count, tile = self.slots.shape[:2]

        @pl.when(step >= count)
        def _():
            self.copy(step - count).wait()

        self.slots[lax.rem(step, count)] = lax.dot_general(
            self.left[:, aligned(self.first + step, tile)],
            self.split[...],
            TN,
            preferred_element_type=F32,
        )
        self.copy(step).start()

    def finish(self):
        for step in range(max(0, self.steps - self.slots.shape[0]), self.steps):
            self.copy(step).wait()


def loop(steps, run):
    def one(step, carry):
        run(step)
        return carry

    lax.fori_loop(0, steps, one, 0)


def units_kernel(count, steps, *refs):
    grads, refs = refs[:count], refs[count:]
    w_ref, out_ref, split_ref, rows_ref, slots, sems = refs
    reader = Reader(w_ref, slots, sems, 0, steps)
    reader.begin()
    rows = rows_ref.shape[0]
    block = rows // count
    for position, value in enumerate(in_order(grads, lax.axis_index("din"))):
        rows_ref[position * block : (position + 1) * block, :] = value
    high, low = halves(rows_ref[...])
    split_ref[...] = jnp.concatenate([high, low, high], axis=0)

    def run(step):
        tile = slots.shape[1]
        out_ref[:, aligned(step, tile)] = multiply(split_ref, rows, reader.take(step))

    loop(steps, run)


def in_vmem(count=1):
    return [pl.BlockSpec(memory_space=pltpu.VMEM)] * count


def in_hbm(count=1):
    return [pl.BlockSpec(memory_space=pltpu.MemorySpace.HBM)] * count


def ring(slots, tile, width):
    return [pltpu.VMEM((slots, tile, width), F32), pltpu.SemaphoreType.DMA((slots,))]


def units(grads, weight, steps, tile):
    width = weight.shape[1]
    count = len(grads)
    rows = sum(piece.shape[0] for piece in grads)
    return pl.pallas_call(
        functools.partial(units_kernel, count, steps),
        out_shape=[
            pltpu.VMEM((rows, steps * tile), F32),
            pltpu.VMEM((3 * rows, width), BF16),
        ],
        in_specs=in_vmem(count) + in_hbm(),
        out_specs=in_vmem(2),
        scratch_shapes=[pltpu.VMEM((rows, width), F32)] + ring(READ_SLOTS, tile, width),
        compiler_params=pltpu.CompilerParams(vmem_limit_bytes=28 << 20),
        name="units",
    )(*grads, weight)


def both_kernel(count, steps, *refs):
    pieces, refs = refs[:count], refs[count:]
    (
        split_ref, begun_ref, w_ref, total_ref, left_ref, out_ref, rows_ref,
        read_slots, read_sems, write_slots, write_sems,
    ) = refs
    tile = read_slots.shape[1]
    rows = rows_ref.shape[0]
    begun = begun_ref.shape[1]
    reader = Reader(w_ref, read_slots, read_sems, begun // tile, steps)
    reader.begin()
    block = rows // count
    for position, value in enumerate(in_order(pieces, lax.axis_index("dout") // 2)):
        rows_ref[position * block : (position + 1) * block, :] = value
    high, low = halves(rows_ref[...])
    left_ref[...] = jnp.concatenate([high, high, low], axis=0)
    writer = Writer(left_ref, split_ref, out_ref, write_slots, write_sems, 0, steps)

    def run(step):
        writer.make(step)
        total_ref[:, aligned(begun // tile + step, tile)] = multiply(
            split_ref, rows, reader.take(step)
        )

    loop(steps, run)
    total_ref[:, :begun] = begun_ref[...]
    writer.finish()


def both(pieces, split, begun, weight, tile):
    depth, width = weight.shape
    count = len(pieces)
    rows = begun.shape[0]
    steps = (depth - begun.shape[1]) // tile
    return pl.pallas_call(
        functools.partial(both_kernel, count, steps),
        out_shape=[
            pltpu.VMEM((rows, depth), F32),
            pltpu.VMEM((3 * rows, depth), BF16),
            jax.ShapeDtypeStruct((depth, width), F32),
        ],
        in_specs=in_vmem(count + 2) + in_hbm(),
        out_specs=in_vmem(2) + in_hbm(),
        scratch_shapes=[pltpu.VMEM((rows, depth), F32)]
        + ring(READ_SLOTS, tile, width)
        + ring(WRITE_SLOTS, tile, width),
        compiler_params=pltpu.CompilerParams(vmem_limit_bytes=32 << 20),
        name="both",
    )(*pieces, split, begun, weight)


def outer_kernel(first, steps, left_ref, split_ref, begun_ref, out_ref, slots, sems):
    del begun_ref
    writer = Writer(left_ref, split_ref, out_ref, slots, sems, first, steps)
    loop(steps, writer.make)
    writer.finish()


def outer(left, split, buffer, first, steps, tile):
    depth, width = left.shape[1], split.shape[1]
    return pl.pallas_call(
        functools.partial(outer_kernel, first, steps),
        out_shape=jax.ShapeDtypeStruct((depth, width), F32),
        in_specs=in_vmem(2) + in_hbm(),
        out_specs=in_hbm()[0],
        scratch_shapes=ring(min(steps, WRITE_SLOTS), tile, width),
        input_output_aliases={2: 0},
        compiler_params=pltpu.CompilerParams(vmem_limit_bytes=24 << 20),
    )(left, split, buffer)


def bit_of(axis, distance):
    return (lax.axis_index(axis) // distance) % 2 == 1


def joined(value, n_out, distance):
    other = swap(value, "dout", n_out, distance)
    return jnp.where(
        bit_of("dout", distance),
        jnp.concatenate([other, value], 0),
        jnp.concatenate([value, other], 0),
    )


def halved(value, n_out, distance):
    half = value.shape[0] // 2
    upper = bit_of("dout", distance)
    keep = jnp.where(upper, value[half:], value[:half])
    give = jnp.where(upper, value[:half], value[half:])
    return keep + swap(give, "dout", n_out, distance)


def body(n_in, n_out, inputs, out_grad, weight):
    depth = weight.shape[0]
    rounds = n_out.bit_length() - 1
    weight = pltpu.with_memory_space_constraint(weight, pltpu.MemorySpace.HBM)
    grads = [out_grad] + [swap(out_grad, "din", n_in, s) for s in range(1, n_in)]
    pair = joined(inputs, n_out, 1)
    pieces = [pair]
    pieces += [swap(pair, "dout", n_out, 2 * s) for s in range(1, n_out // 2)]
    begun, split = units(grads, weight, depth // UNITS_TILE // 2, UNITS_TILE)
    total, left, weight_grad = both(pieces, split, begun, weight, BOTH_TILE)
    parts = depth // OUTER_TILE
    first = parts // 2
    rest = parts - first
    for r in range(rounds):
        total = halved(total, n_out, n_out >> (r + 1))
        steps = (rest + rounds - 1 - r) // (rounds - r)
        rest -= steps
        weight_grad = outer(left, split, weight_grad, first, steps, OUTER_TILE)
        first += steps
    return (total, weight_grad)


def power_of_two(value):
    return value & (value - 1) == 0


def solution(mesh):
    n_in, n_out = mesh.shape["din"], mesh.shape["dout"]
    shaped = (
        power_of_two(n_in) and power_of_two(n_out) and n_in <= 8 and 4 <= n_out <= 8
    )

    def run(inputs, out_grad, weight):
        depth, width = weight.shape
        fits = (
            inputs.shape[0] * n_out <= 64
            and depth % (2 * UNITS_TILE) == 0
            and depth >= 8 * UNITS_TILE
            and width % 128 == 0
        )
        if not (shaped and fits):
            return plain_body(inputs, out_grad, weight)
        return body(n_in, n_out, inputs, out_grad, weight)

    placed = (P("dout", "din"), P("din", "dout"), P("din", "dout"))
    return jax.shard_map(
        run,
        mesh=mesh,
        in_specs=placed,
        out_specs=(P("dout", "din"), P("din", "dout")),
        check_vma=False,
    )
```

time: 125 us -> 52 us (0.42)
  matrix products: 56.2 us -> 0 us
  blocking collectives: 38.5 us -> 0 us
  Pallas kernels: 0 us -> 27.8 us
  starting transfers between devices: 0.04 us -> 15 us
  between operations: 14.7 us -> 0.76 us
  waiting for transfers between devices: 12.7 us -> 5.8 us
  other arithmetic: 0 us -> 1.5 us
  local copies, waits for them, and re-layouts: 2.22 us -> 0.81 us
    dot_general x2 -> x0, matrix products: 56.2 us -> none  [the longest x1 29.5 us: contract_units(): lax.dot_general(left, right, (((1,), (1,)), ((), ())), precision=lax.Prec...]
    all_gather x2 -> x0, blocking collectives: 38.5 us -> none  [the longest x1 31.2 us: body(): lax.all_gather(inputs, 'dout', axis=0, tiled=True)]
    pallas_call x0 -> x5, Pallas kernels: none -> 27.8 us  [the longest x1 13.2 us: both(): pl.pallas_call(functools.partial(both_kernel, count, steps), out_shape=[p...]
    ppermute x0 -> x10, starting transfers between devices: none -> 15 us  [swap(): return lax.ppermute(value, axis, [(i, i ^ distance) for i in range(size)])]
    unnamed x2 -> x0, waiting for transfers between devices: 12.7 us -> none
    ppermute x0 -> x10, waiting for transfers between devices: none -> 5.8 us  [swap(): return lax.ppermute(value, axis, [(i, i ^ distance) for i in range(size)])]
    unnamed x8 -> x2, local copies, waits for them, and re-layouts: 2.22 us -> 0.81 us
  transfers between devices with their start and end apart: 1 -> 10, of which waited for: 1 -> 3; matrix products, arithmetic and copies ran while one was open for 22% -> 2% of each run, Pallas kernels for 0% -> 28%
where the time goes in v1:
time: 52 us; the launch traced here: 51.7 us
  Pallas kernels  27.8 us (53%)
  starting transfers between devices  15 us (29%)
  waiting for transfers between devices  5.8 us (11%)
  other arithmetic  1.5 us (3%)
  local copies, waits for them, and re-layouts  0.81 us (2%)
  between operations  0.76 us (1%)
    ppermute x10, starting transfers between devices, swap(): return lax.ppermute(value, axis, [(i, i ^ distance) for i in range(size)])  15 us
    pallas_call x1, Pallas kernels, both(): pl.pallas_call(functools.partial(both_kernel, count, steps), out_shape=[p...  13.2 us
    pallas_call x3, Pallas kernels, outer(): pl.pallas_call(functools.partial(outer_kernel, first, steps), out_shape=j...  8.07 us
    pallas_call x1, Pallas kernels, units(): pl.pallas_call(functools.partial(units_kernel, count, steps), out_shape=[...  6.57 us
    ppermute x10, waiting for transfers between devices, swap(): return lax.ppermute(value, axis, [(i, i ^ distance) for i in range(size)])  5.8 us
  transfers between devices with their start and end apart: 10, of which 3 were waited for; matrix products, arithmetic and copies ran while one was open for 2% of the time, Pallas kernels for 28%

profile of v1, /device:TPU:0, one launch (start us, length us, event | category | flops | bytes accessed | tf_op | source)
XLA Modules:
  0.0 51.7 jit_solution(1595556642767492057)
XLA Ops:
  0.6 3.1 %collective-permute-start = (f32[2,2048]{1,0:T(2,128)}, f32[2,2048]{1,0:T(2,128)S(1)}, u32[]{:S(2)}, u32[]{:S(2)}) collective-permute-start(f32[2,2048]{1,0:T(2,128)} %param.3), channel_id=1, source_target_pairs={{0,1},{1,0},{2,3},{3,2},{4,5},{5,4},{6,7},{7,6},{8,9},{9,8},{10,11... | collective-permute-start | bytes 49160 | tf_op jit(solution)/shard_map/ppermute | solution.py:43
  3.7 0.0 collective-permute-start.4
  3.7 1.5 %collective-permute-start.5 = (f32[4,3584]{1,0:T(4,128)}, f32[4,3584]{1,0:T(4,128)S(1)}, u32[]{:S(2)}, u32[]{:S(2)}) collective-permute-start(f32[4,3584]{1,0:T(4,128)} %refs_0_.1), channel_id=1, source_target_pairs={{0,16},{8,24},{16,0},{24,8},{1,17},{9,25},{17,1},{25,9},{2,18},{10... | collective-permute-start | bytes 172040 | tf_op jit(solution)/shard_map/ppermute | solution.py:43
  5.2 0.4 collective-permute-start.6
  5.6 0.1 collective-permute-done
  5.6 0.8 %maximum_select_fusion.refs_0_ = f32[4,2048]{1,0:T(4,128)S(1)} fusion(f32[2,2048]{1,0:T(2,128)} %param.3, f32[2,2048]{1,0:T(2,128)S(1)} %collective-permute-done, pred[]{:T(512)S(6)} %eq.15), kind=kLoop, calls=%fused_computation.2 | loop fusion | flops 24576 | bytes 65537 | tf_op jit(solution)/shard_map/jit(_where)/select_n | solution.py:266
  6.4 2.1 %collective-permute-start.1 = (f32[4,2048]{1,0:T(4,128)S(1)}, f32[4,2048]{1,0:T(4,128)S(1)}, u32[]{:S(2)}, u32[]{:S(2)}) collective-permute-start(f32[4,2048]{1,0:T(4,128)S(1)} %maximum_select_fusion.refs_0_), channel_id=1, source_target_pairs={{0,2},{1,3},{2,0},{3,1},{4,6},{5,7},{6,4},{7,5},{8,10},{9,11},{10,... | collective-permute-start | bytes 98312 | tf_op jit(solution)/shard_map/ppermute | solution.py:43
  8.6 2.6 %collective-permute-start.2 = (f32[4,2048]{1,0:T(4,128)S(1)}, f32[4,2048]{1,0:T(4,128)S(1)}, u32[]{:S(2)}, u32[]{:S(2)}) collective-permute-start(f32[4,2048]{1,0:T(4,128)S(1)} %maximum_select_fusion.refs_0_), channel_id=1, source_target_pairs={{0,4},{1,5},{2,6},{3,7},{4,0},{5,1},{6,2},{7,3},{8,12},{9,13},{10,... | collective-permute-start | bytes 98312 | tf_op jit(solution)/shard_map/ppermute | solution.py:43
  11.2 0.0 collective-permute-done.4.refs_1_
  11.2 0.0 collective-permute-done.6.refs_3_
  11.2 0.0 copy-start
  11.2 0.8 %copy-done = f32[4,3584]{1,0:T(4,128)S(1)} copy-done((f32[4,3584]{1,0:T(4,128)S(1)}, f32[4,3584]{1,0:T(4,128)}, u32[]{:S(2)}) %copy-start) | copy-done | bytes 57368
  12.0 6.6 %units.1 = (f32[16,1024]{1,0:T(8,128)S(1)}, bf16[48,3584]{1,0:T(8,128)(2,1)S(1)}) custom-call(f32[4,3584]{1,0:T(4,128)S(1)} %copy-done, f32[4,3584]{1,0:T(4,128)S(1)} %collective-permute-done.4.refs_1_, f32[4,3584]{1,0:T(4,128)S(1)} %collective-permute-done.5.refs_2_, f32[4,3584]{1,0:T(4,128)S(1)} %collective-permute-done.6.refs_3_, f32[2048,3584]{1,0:T(8,128)} %refs_6_.1), custom_call_target="tpu_custom_call" | custom-call | tf_op jit(solution)/shard_map/units/pallas_call | solution.py:175
  18.6 0.0 collective-permute-done.2.refs_2_
  18.6 13.2 %both.1 = (f32[16,2048]{1,0:T(8,128)S(1)}, bf16[48,2048]{1,0:T(8,128)(2,1)S(1)}, f32[2048,3584]{1,0:T(8,128)}) custom-call(f32[4,2048]{1,0:T(4,128)S(1)} %maximum_select_fusion.refs_0_, f32[4,2048]{1,0:T(4,128)S(1)} %collective-permute-done.1.refs_1_, f32[4,2048]{1,0:T(4,128)S(1)} %collective-permute-done.2.refs_2_, ...), custom_call_target="tpu_custom_call" | custom-call | tf_op jit(solution)/shard_map/both/pallas_call | solution.py:223
  31.8 2.0 %collective-permute-start.7 = (f32[8,2048]{1,0:T(8,128)S(1)}, f32[8,2048]{1,0:T(8,128)S(1)}, u32[]{:S(2)}, u32[]{:S(2)}) collective-permute-start(f32[8,2048]{1,0:T(8,128)S(1)} %slice_select_fusion), channel_id=1, source_target_pairs={{0,4},{1,5},{2,6},{3,7},{4,0},{5,1},{6,2},{7,3},{8,12},{9,13},{10,... | collective-permute-start | bytes 196616 | tf_op jit(solution)/shard_map/ppermute | solution.py:43
  33.8 3.3 %collective-permute-done.7 = f32[8,2048]{1,0:T(8,128)S(1)} collective-permute-done((f32[8,2048]{1,0:T(8,128)S(1)}, f32[8,2048]{1,0:T(8,128)S(1)}, u32[]{:S(2)}, u32[]{:S(2)}) %collective-permute-start.7) | collective-permute-done | bytes 65568 | tf_op jit(solution)/shard_map/ppermute | solution.py:43
  37.1 1.5 %collective-permute-start.8 = (f32[4,2048]{1,0:T(4,128)S(1)}, f32[4,2048]{1,0:T(4,128)S(1)}, u32[]{:S(2)}, u32[]{:S(2)}) collective-permute-start(f32[4,2048]{1,0:T(4,128)S(1)} %slice_select_fusion.1), channel_id=1, source_target_pairs={{0,2},{1,3},{2,0},{3,1},{4,6},{5,7},{6,4},{7,5},{8,10},{9,11},{10,... | collective-permute-start | bytes 98312 | tf_op jit(solution)/shard_map/ppermute | solution.py:43
  38.6 2.5 %collective-permute-done.8 = f32[4,2048]{1,0:T(4,128)S(1)} collective-permute-done((f32[4,2048]{1,0:T(4,128)S(1)}, f32[4,2048]{1,0:T(4,128)S(1)}, u32[]{:S(2)}, u32[]{:S(2)}) %collective-permute-start.8) | collective-permute-done | bytes 32800 | tf_op jit(solution)/shard_map/ppermute | solution.py:43
  41.1 1.8 %collective-permute-start.9 = (f32[2,2048]{1,0:T(2,128)S(1)}, f32[2,2048]{1,0:T(2,128)S(1)}, u32[]{:S(2)}, u32[]{:S(2)}) collective-permute-start(f32[2,2048]{1,0:T(2,128)S(1)} %broadcast_select_fusion), channel_id=1, source_target_pairs={{0,1},{1,0},{2,3},{3,2},{4,5},{5,4},{6,7},{7,6},{8,9},{9,8},{10,11... | collective-permute-start | bytes 49160 | tf_op jit(solution)/shard_map/ppermute | solution.py:43
  43.0 2.9 %shard_map.50.begun_ref = f32[2048,3584]{1,0:T(8,128)} custom-call(bf16[48,2048]{1,0:T(8,128)(2,1)S(1)} %get-tuple-element.10.left_ref, bf16[48,3584]{1,0:T(8,128)(2,1)S(1)} %get-tuple-element.7.refs_4_.split_ref, f32[2048,3584]{1,0:T(8,128)} %get-tuple-element.11.begun_ref), custom_call_target="tpu_custom_call", output_to_operand_aliasing={{}: (2, {})} | custom-call | tf_op jit(solution)/shard_map/pallas_call | solution.py:249
  45.8 2.9 %shard_map.51.begun_ref = f32[2048,3584]{1,0:T(8,128)} custom-call(bf16[48,2048]{1,0:T(8,128)(2,1)S(1)} %get-tuple-element.10.left_ref, bf16[48,3584]{1,0:T(8,128)(2,1)S(1)} %get-tuple-element.7.refs_4_.split_ref, f32[2048,3584]{1,0:T(8,128)} %shard_map.50.begun_ref), custom_call_target="tpu_custom_call", output_to_operand_aliasing={{}: (2, {})} | custom-call | tf_op jit(solution)/shard_map/pallas_call | solution.py:249
  48.8 2.3 %shard_map.52 = f32[2048,3584]{1,0:T(8,128)} custom-call(bf16[48,2048]{1,0:T(8,128)(2,1)S(1)} %get-tuple-element.10.left_ref, bf16[48,3584]{1,0:T(8,128)(2,1)S(1)} %get-tuple-element.7.refs_4_.split_ref, f32[2048,3584]{1,0:T(8,128)} %shard_map.51.begun_ref), custom_call_target="tpu_custom_call", output_to_operand_aliasing={{}: (2, {})} | custom-call | tf_op jit(solution)/shard_map/pallas_call | solution.py:249
  51.1 0.6 %select_add_fusion.2 = f32[2,2048]{1,0:T(2,128)} fusion(f32[2,2048]{1,0:T(2,128)S(1)} %collective-permute-done.9, pred[]{:T(512)S(6)} %eq.15, f32[4,2048]{1,0:T(4,128)S(1)} %select_add_fusion.1), kind=kLoop, calls=%fused_computation.5 | loop fusion | flops 8192 | bytes 65537 | tf_op jit(solution)/shard_map/add | solution.py:278
  (10 shorter events, 0.1 us)
Async XLA Ops:
  0.6 5.0 %collective-permute-start = (f32[2,2048]{1,0:T(2,128)}, f32[2,2048]{1,0:T(2,128)S(1)}, u32[]{:S(2)}, u32[]{:S(2)}) collective-permute-start(f32[2,2048]{1,0:T(2,128)} %param.3), channel_id=1, source_target_pairs={{0,1},{1,0},{2,3},{3,2},{4,5},{5,4},{6,7},{7,6},{8,9},{9,8},{10,11... | collective-permute-start | bytes 49160 | tf_op jit(solution)/shard_map/ppermute | solution.py:43
  3.7 7.5 %collective-permute-start.4 = (f32[4,3584]{1,0:T(4,128)}, f32[4,3584]{1,0:T(4,128)S(1)}, u32[]{:S(2)}, u32[]{:S(2)}) collective-permute-start(f32[4,3584]{1,0:T(4,128)} %refs_0_.1), channel_id=1, source_target_pairs={{0,8},{8,0},{16,24},{24,16},{1,9},{9,1},{17,25},{25,17},{2,10},{10... | collective-permute-start | bytes 172040 | tf_op jit(solution)/shard_map/ppermute | solution.py:43
  3.7 7.5 %collective-permute-start.5 = (f32[4,3584]{1,0:T(4,128)}, f32[4,3584]{1,0:T(4,128)S(1)}, u32[]{:S(2)}, u32[]{:S(2)}) collective-permute-start(f32[4,3584]{1,0:T(4,128)} %refs_0_.1), channel_id=1, source_target_pairs={{0,16},{8,24},{16,0},{24,8},{1,17},{9,25},{17,1},{25,9},{2,18},{10... | collective-permute-start | bytes 172040 | tf_op jit(solution)/shard_map/ppermute | solution.py:43
  5.2 6.0 %collective-permute-start.6 = (f32[4,3584]{1,0:T(4,128)}, f32[4,3584]{1,0:T(4,128)S(1)}, u32[]{:S(2)}, u32[]{:S(2)}) collective-permute-start(f32[4,3584]{1,0:T(4,128)} %refs_0_.1), channel_id=1, source_target_pairs={{0,24},{8,16},{16,8},{24,0},{1,25},{9,17},{17,9},{25,1},{2,26},{10... | collective-permute-start | bytes 172040 | tf_op jit(solution)/shard_map/ppermute | solution.py:43
  6.4 12.2 %collective-permute-start.1 = (f32[4,2048]{1,0:T(4,128)S(1)}, f32[4,2048]{1,0:T(4,128)S(1)}, u32[]{:S(2)}, u32[]{:S(2)}) collective-permute-start(f32[4,2048]{1,0:T(4,128)S(1)} %maximum_select_fusion.refs_0_), channel_id=1, source_target_pairs={{0,2},{1,3},{2,0},{3,1},{4,6},{5,7},{6,4},{7,5},{8,10},{9,11},{10,... | collective-permute-start | bytes 98312 | tf_op jit(solution)/shard_map/ppermute | solution.py:43
  8.6 10.0 %collective-permute-start.2 = (f32[4,2048]{1,0:T(4,128)S(1)}, f32[4,2048]{1,0:T(4,128)S(1)}, u32[]{:S(2)}, u32[]{:S(2)}) collective-permute-start(f32[4,2048]{1,0:T(4,128)S(1)} %maximum_select_fusion.refs_0_), channel_id=1, source_target_pairs={{0,4},{1,5},{2,6},{3,7},{4,0},{5,1},{6,2},{7,3},{8,12},{9,13},{10,... | collective-permute-start | bytes 98312 | tf_op jit(solution)/shard_map/ppermute | solution.py:43
  11.2 7.4 %collective-permute-start.3 = (f32[4,2048]{1,0:T(4,128)S(1)}, f32[4,2048]{1,0:T(4,128)S(1)}, u32[]{:S(2)}, u32[]{:S(2)}) collective-permute-start(f32[4,2048]{1,0:T(4,128)S(1)} %maximum_select_fusion.refs_0_), channel_id=1, source_target_pairs={{0,6},{1,7},{2,4},{3,5},{4,2},{5,3},{6,0},{7,1},{8,14},{9,15},{10,... | collective-permute-start | bytes 98312 | tf_op jit(solution)/shard_map/ppermute | solution.py:43
  11.2 0.8 %copy-start = (f32[4,3584]{1,0:T(4,128)S(1)}, f32[4,3584]{1,0:T(4,128)}, u32[]{:S(2)}) copy-start(f32[4,3584]{1,0:T(4,128)} %refs_0_.1) | copy-start | bytes 172036
  31.8 5.2 %collective-permute-start.7 = (f32[8,2048]{1,0:T(8,128)S(1)}, f32[8,2048]{1,0:T(8,128)S(1)}, u32[]{:S(2)}, u32[]{:S(2)}) collective-permute-start(f32[8,2048]{1,0:T(8,128)S(1)} %slice_select_fusion), channel_id=1, source_target_pairs={{0,4},{1,5},{2,6},{3,7},{4,0},{5,1},{6,2},{7,3},{8,12},{9,13},{10,... | collective-permute-start | bytes 196616 | tf_op jit(solution)/shard_map/ppermute | solution.py:43
  37.1 4.0 %collective-permute-start.8 = (f32[4,2048]{1,0:T(4,128)S(1)}, f32[4,2048]{1,0:T(4,128)S(1)}, u32[]{:S(2)}, u32[]{:S(2)}) collective-permute-start(f32[4,2048]{1,0:T(4,128)S(1)} %slice_select_fusion.1), channel_id=1, source_target_pairs={{0,2},{1,3},{2,0},{3,1},{4,6},{5,7},{6,4},{7,5},{8,10},{9,11},{10,... | collective-permute-start | bytes 98312 | tf_op jit(solution)/shard_map/ppermute | solution.py:43
  41.1 9.9 %collective-permute-start.9 = (f32[2,2048]{1,0:T(2,128)S(1)}, f32[2,2048]{1,0:T(2,128)S(1)}, u32[]{:S(2)}, u32[]{:S(2)}) collective-permute-start(f32[2,2048]{1,0:T(2,128)S(1)} %broadcast_select_fusion), channel_id=1, source_target_pairs={{0,1},{1,0},{2,3},{3,2},{4,5},{5,4},{6,7},{7,6},{8,9},{9,8},{10,11... | collective-permute-start | bytes 49160 | tf_op jit(solution)/shard_map/ppermute | solution.py:43

commit v2 on v1

--- a/solution.py
+++ b/solution.py
@@ -14,10 +14,10 @@
 NT = (((1,), (1,)), ((), ()))
 
 UNITS_TILE = 256
-BOTH_TILE = 128
 OUTER_TILE = 128
 READ_SLOTS = 4
-WRITE_SLOTS = 3
+WRITE_SLOTS = 4
+CUTS = 2
 
 
 def plain_body(inputs, out_grad, weight):
@@ -84,13 +84,14 @@
         for step in range(self.ahead):
             self.copy(step).start()
 
-    def take(self, step):
+    def arrive(self, step):
         self.copy(step).wait()
 
         @pl.when(step + self.ahead < self.steps)
         def _():
             self.copy(step + self.ahead).start()
 
+    def take(self, step):
         return self.slots[lax.rem(step, self.slots.shape[0])]
 
 
@@ -99,34 +100,47 @@
         self.left, self.split, self.out = left_ref, split_ref, out_ref
         self.slots, self.sems = slots, sems
         self.first, self.steps = first, steps
-
-    def copy(self, step):
-        count, tile = self.slots.shape[:2]
+        self.cuts = sems.shape[1]
+
+    def copies(self, step):
+        count, tile, width = self.slots.shape
         slot = lax.rem(step, count)
-        return pltpu.make_async_copy(
-            self.slots.at[slot],
-            self.out.at[aligned(self.first + step, tile), :],
-            self.sems.at[slot],
-        )
+        part = width // self.cuts
+        return [
+            pltpu.make_async_copy(
+                self.slots.at[slot, :, pl.ds(k * part, part)],
+                self.out.at[aligned(self.first + step, tile), pl.ds(k * part, part)],
+                self.sems.at[slot, k],
+            )
+            for k in range(self.cuts)
+        ]
 
     def make(self, step):
-        count, tile = self.slots.shape[:2]
-
-        @pl.when(step >= count)
-        def _():
-            self.copy(step - count).wait()
-
-        self.slots[lax.rem(step, count)] = lax.dot_general(
-            self.left[:, aligned(self.first + step, tile)],
-            self.split[...],
-            TN,
-            preferred_element_type=F32,
-        )
-        self.copy(step).start()
+        count, tile, width = self.slots.shape
+        part = width // self.cuts
+        if count < self.steps:
+
+            @pl.when(step >= count)
+            def _():
+                for copy in self.copies(step - count):
+                    copy.wait()
+
+        left = self.left[:, aligned(self.first + step, tile)]
+        for k, copy in enumerate(self.copies(step)):
+            self.slots[lax.rem(step, count), :, k * part : (k + 1) * part] = (
+                lax.dot_general(
+                    left,
+                    self.split[:, k * part : (k + 1) * part],
+                    TN,
+                    preferred_element_type=F32,
+                )
+            )
+            copy.start()
 
     def finish(self):
         for step in range(max(0, self.steps - self.slots.shape[0]), self.steps):
-            self.copy(step).wait()
+            for copy in self.copies(step):
+                copy.wait()
 
 
 def loop(steps, run):
@@ -151,6 +165,7 @@
 
     def run(step):
         tile = slots.shape[1]
+        reader.arrive(step)
         out_ref[:, aligned(step, tile)] = multiply(split_ref, rows, reader.take(step))
 
     loop(steps, run)
@@ -164,8 +179,11 @@
     return [pl.BlockSpec(memory_space=pltpu.MemorySpace.HBM)] * count
 
 
-def ring(slots, tile, width):
-    return [pltpu.VMEM((slots, tile, width), F32), pltpu.SemaphoreType.DMA((slots,))]
+def ring(slots, tile, width, *cuts):
+    return [
+        pltpu.VMEM((slots, tile, width), F32),
+        pltpu.SemaphoreType.DMA((slots, *cuts)),
+    ]
 
 
 def units(grads, weight, steps, tile):
@@ -186,88 +204,83 @@
     )(*grads, weight)
 
 
-def both_kernel(count, steps, *refs):
+def outer_kernel(count, first, steps, *refs):
     pieces, refs = refs[:count], refs[count:]
-    (
-        split_ref, begun_ref, w_ref, total_ref, left_ref, out_ref, rows_ref,
-        read_slots, read_sems, write_slots, write_sems,
-    ) = refs
-    tile = read_slots.shape[1]
-    rows = rows_ref.shape[0]
-    begun = begun_ref.shape[1]
-    reader = Reader(w_ref, read_slots, read_sems, begun // tile, steps)
-    reader.begin()
-    block = rows // count
-    for position, value in enumerate(in_order(pieces, lax.axis_index("dout") // 2)):
-        rows_ref[position * block : (position + 1) * block, :] = value
-    high, low = halves(rows_ref[...])
-    left_ref[...] = jnp.concatenate([high, high, low], axis=0)
-    writer = Writer(left_ref, split_ref, out_ref, write_slots, write_sems, 0, steps)
-
-    def run(step):
-        writer.make(step)
-        total_ref[:, aligned(begun // tile + step, tile)] = multiply(
-            split_ref, rows, reader.take(step)
-        )
-
-    loop(steps, run)
-    total_ref[:, :begun] = begun_ref[...]
+    split_ref, left_ref, out_ref, slots, sems, *rows_ref = refs
+    if count:
+        rows = rows_ref[0].shape[0]
+        block = rows // count
+        for position, value in enumerate(in_order(pieces, lax.axis_index("dout") // 2)):
+            rows_ref[0][position * block : (position + 1) * block, :] = value
+        high, low = halves(rows_ref[0][...])
+        left_ref[...] = jnp.concatenate([high, high, low], axis=0)
+    writer = Writer(left_ref, split_ref, out_ref, slots, sems, first, steps)
+    loop(steps, writer.make)
     writer.finish()
 
 
-def both(pieces, split, begun, weight, tile):
-    depth, width = weight.shape
+def later_kernel(first, steps, split_ref, left_ref, begun_ref, *refs):
+    del begun_ref
+    outer_kernel(0, first, steps, split_ref, left_ref, *refs)
+
+
+def outer_first(pieces, split, steps, tile):
+    depth, width = pieces[0].shape[1], split.shape[1]
     count = len(pieces)
-    rows = begun.shape[0]
-    steps = (depth - begun.shape[1]) // tile
+    rows = split.shape[0] // 3
     return pl.pallas_call(
-        functools.partial(both_kernel, count, steps),
+        functools.partial(outer_kernel, count, 0, steps),
         out_shape=[
-            pltpu.VMEM((rows, depth), F32),
             pltpu.VMEM((3 * rows, depth), BF16),
             jax.ShapeDtypeStruct((depth, width), F32),
         ],
-        in_specs=in_vmem(count + 2) + in_hbm(),
-        out_specs=in_vmem(2) + in_hbm(),
-        scratch_shapes=[pltpu.VMEM((rows, depth), F32)]
-        + ring(READ_SLOTS, tile, width)
-        + ring(WRITE_SLOTS, tile, width),
-        compiler_params=pltpu.CompilerParams(vmem_limit_bytes=32 << 20),
-        name="both",
-    )(*pieces, split, begun, weight)
-
-
-def outer_kernel(first, steps, left_ref, split_ref, begun_ref, out_ref, slots, sems):
-    del begun_ref
-    writer = Writer(left_ref, split_ref, out_ref, slots, sems, first, steps)
-    loop(steps, writer.make)
-    writer.finish()
+        in_specs=in_vmem(count + 1),
+        out_specs=in_vmem() + in_hbm(),
+        scratch_shapes=ring(min(steps, WRITE_SLOTS), tile, width, CUTS)
+        + [pltpu.VMEM((rows, depth), F32)],
+        compiler_params=pltpu.CompilerParams(vmem_limit_bytes=24 << 20),
+        name="outer_0",
+    )(*pieces, split)
 
 
 def outer(left, split, buffer, first, steps, tile):
     depth, width = left.shape[1], split.shape[1]
     return pl.pallas_call(
-        functools.partial(outer_kernel, first, steps),
+        functools.partial(later_kernel, first, steps),
         out_shape=jax.ShapeDtypeStruct((depth, width), F32),
         in_specs=in_vmem(2) + in_hbm(),
         out_specs=in_hbm()[0],
-        scratch_shapes=ring(min(steps, WRITE_SLOTS), tile, width),
+        scratch_shapes=ring(min(steps, WRITE_SLOTS), tile, width, CUTS),
         input_output_aliases={2: 0},
         compiler_params=pltpu.CompilerParams(vmem_limit_bytes=24 << 20),
-    )(left, split, buffer)
+    )(split, left, buffer)
+
+
+def join_kernel(own_ref, other_ref, out_ref):
+    half = own_ref.shape[0]
+    upper = lax.axis_index("dout") % 2
+    own, other = own_ref[...], other_ref[...]
+    out_ref[:half, :] = jnp.where(upper == 1, other, own)
+    out_ref[half:, :] = jnp.where(upper == 1, own, other)
+
+
+def join(own, other, cost):
+    rows, width = own.shape
+    return pl.pallas_call(
+        join_kernel,
+        out_shape=jax.ShapeDtypeStruct((2 * rows, width), F32),
+        in_specs=in_vmem(2),
+        out_specs=in_vmem()[0],
+        cost_estimate=pl.CostEstimate(
+            flops=cost, bytes_accessed=0, transcendentals=0
+        ),
+        compiler_params=pltpu.CompilerParams(vmem_limit_bytes=2 << 20),
+        name="join",
+    )(own, other)
 
 
 def bit_of(axis, distance):
     return (lax.axis_index(axis) // distance) % 2 == 1
-
-
-def joined(value, n_out, distance):
-    other = swap(value, "dout", n_out, distance)
-    return jnp.where(
-        bit_of("dout", distance),
-        jnp.concatenate([other, value], 0),
-        jnp.concatenate([value, other], 0),
-    )
 
 
 def halved(value, n_out, distance):
@@ -283,19 +296,19 @@
     rounds = n_out.bit_length() - 1
     weight = pltpu.with_memory_space_constraint(weight, pltpu.MemorySpace.HBM)
     grads = [out_grad] + [swap(out_grad, "din", n_in, s) for s in range(1, n_in)]
-    pair = joined(inputs, n_out, 1)
+    pair = join(inputs, swap(inputs, "dout", n_out, 1), 100000000000)
     pieces = [pair]
     pieces += [swap(pair, "dout", n_out, 2 * s) for s in range(1, n_out // 2)]
-    begun, split = units(grads, weight, depth // UNITS_TILE // 2, UNITS_TILE)
-    total, left, weight_grad = both(pieces, split, begun, weight, BOTH_TILE)
-    parts = depth // OUTER_TILE
-    first = parts // 2
-    rest = parts - first
+    total, split = units(grads, weight, depth // UNITS_TILE, UNITS_TILE)
+    first, rest = 0, depth // OUTER_TILE
     for r in range(rounds):
         total = halved(total, n_out, n_out >> (r + 1))
         steps = (rest + rounds - 1 - r) // (rounds - r)
         rest -= steps
-        weight_grad = outer(left, split, weight_grad, first, steps, OUTER_TILE)
+        if r == 0:
+            left, weight_grad = outer_first(pieces, split, steps, OUTER_TILE)
+        else:
+            weight_grad = outer(left, split, weight_grad, first, steps, OUTER_TILE)
         first += steps
     return (total, weight_grad)
 

time: 52 us -> 47.9 us (0.921)
  Pallas kernels: 27.8 us -> 23.3 us
  waiting for transfers between devices: 5.8 us -> 8.02 us
  other arithmetic: 1.5 us -> 0.68 us
  starting transfers between devices: 15 us -> 14.2 us
    pallas_call x4, Pallas kernels: 21.2 us -> 12.4 us  [the longest x2 7.87 us: outer(): pl.pallas_call(functools.partial(later_kernel, first, steps), out_shape=j...]
    pallas_call x1, Pallas kernels: 6.57 us -> 10.9 us  [units(): pl.pallas_call(functools.partial(units_kernel, count, steps), out_shape=[...]
    ppermute x10, waiting for transfers between devices: 5.8 us -> 8.02 us  [swap(): return lax.ppermute(value, axis, [(i, i ^ distance) for i in range(size)])]
    select_n x1 -> x0, other arithmetic: 0.82 us -> none  [joined(): jnp.where(bit_of('dout', distance), jnp.concatenate([other, value], 0), j...]
    ppermute x10, starting transfers between devices: 15 us -> 14.2 us  [swap(): return lax.ppermute(value, axis, [(i, i ^ distance) for i in range(size)])]
  transfers between devices with their start and end apart: 10 -> 10, of which waited for: 3 -> 4; matrix products, arithmetic and copies ran while one was open for 2% -> 0% of each run, Pallas kernels for 28% -> 26%
where the time goes in v2:
time: 47.9 us; the launch traced here: 47.7 us
  Pallas kernels  23.3 us (49%)
  starting transfers between devices  14.2 us (30%)
  waiting for transfers between devices  8.02 us (17%)
  local copies, waits for them, and re-layouts  0.82 us (2%)
  between operations  0.72 us (2%)
  other arithmetic  0.68 us (1%)
    ppermute x10, starting transfers between devices, swap(): return lax.ppermute(value, axis, [(i, i ^ distance) for i in range(size)])  14.2 us
    pallas_call x1, Pallas kernels, units(): pl.pallas_call(functools.partial(units_kernel, count, steps), out_shape=[...  10.9 us
    ppermute x10, waiting for transfers between devices, swap(): return lax.ppermute(value, axis, [(i, i ^ distance) for i in range(size)])  8.02 us
    pallas_call x2, Pallas kernels, outer(): pl.pallas_call(functools.partial(later_kernel, first, steps), out_shape=j...  7.87 us
    pallas_call x1, Pallas kernels, outer_first(): pl.pallas_call(functools.partial(outer_kernel, count, 0, steps), out_shap...  4.54 us
  transfers between devices with their start and end apart: 10, of which 4 were waited for; matrix products, arithmetic and copies ran while one was open for 0% of the time, Pallas kernels for 26%

profile of v2, /device:TPU:0, one launch (start us, length us, event | category | flops | bytes accessed | tf_op | source)
XLA Modules:
  0.0 47.7 jit_solution(5991563246224665217)
XLA Ops:
  0.6 3.0 %collective-permute-start.1 = (f32[4,3584]{1,0:T(4,128)}, f32[4,3584]{1,0:T(4,128)S(1)}, u32[]{:S(2)}, u32[]{:S(2)}) collective-permute-start(f32[4,3584]{1,0:T(4,128)} %refs_0_.1), channel_id=1, source_target_pairs={{0,16},{8,24},{16,0},{24,8},{1,17},{9,25},{17,1},{25,9},{2,18},{10... | collective-permute-start | bytes 172040 | tf_op jit(solution)/shard_map/ppermute | solution.py:43
  3.7 0.0 collective-permute-start
  3.7 0.2 collective-permute-start.2
  3.9 2.3 %collective-permute-done.1.refs_2_ = f32[4,3584]{1,0:T(4,128)S(1)} collective-permute-done((f32[4,3584]{1,0:T(4,128)}, f32[4,3584]{1,0:T(4,128)S(1)}, u32[]{:S(2)}, u32[]{:S(2)}) %collective-permute-start.1) | collective-permute-done | bytes 57376 | tf_op jit(solution)/shard_map/ppermute | solution.py:43
  6.1 0.0 collective-permute-done.refs_1_
  6.1 1.4 %collective-permute-done.2.refs_3_ = f32[4,3584]{1,0:T(4,128)S(1)} collective-permute-done((f32[4,3584]{1,0:T(4,128)}, f32[4,3584]{1,0:T(4,128)S(1)}, u32[]{:S(2)}, u32[]{:S(2)}) %collective-permute-start.2) | collective-permute-done | bytes 57376 | tf_op jit(solution)/shard_map/ppermute | solution.py:43
  7.5 0.8 %copy-done = f32[4,3584]{1,0:T(4,128)S(1)} copy-done((f32[4,3584]{1,0:T(4,128)S(1)}, f32[4,3584]{1,0:T(4,128)}, u32[]{:S(2)}) %copy-start) | copy-done | bytes 57368
  8.3 10.9 %units.1 = (f32[16,2048]{1,0:T(8,128)S(1)}, bf16[48,3584]{1,0:T(8,128)(2,1)S(1)}) custom-call(f32[4,3584]{1,0:T(4,128)S(1)} %copy-done, f32[4,3584]{1,0:T(4,128)S(1)} %collective-permute-done.refs_1_, f32[4,3584]{1,0:T(4,128)S(1)} %collective-permute-done.1.refs_2_, f32[4,3584]{1,0:T(4,128)S(1)} %collective-permute-done.2.refs_3_, f32[2048,3584]{1,0:T(8,128)} %refs_4_.1), custom_call_target="tpu_custom_call" | custom-call | tf_op jit(solution)/shard_map/units/pallas_call | solution.py:193
  19.2 2.7 %collective-permute-start.3 = (f32[8,2048]{1,0:T(8,128)S(1)}, f32[8,2048]{1,0:T(8,128)S(1)}, u32[]{:S(2)}, u32[]{:S(2)}) collective-permute-start(f32[8,2048]{1,0:T(8,128)S(1)} %slice_select_fusion), channel_id=1, source_target_pairs={{0,4},{1,5},{2,6},{3,7},{4,0},{5,1},{6,2},{7,3},{8,12},{9,13},{10,... | collective-permute-start | bytes 196616 | tf_op jit(solution)/shard_map/ppermute | solution.py:43
  21.9 1.5 %collective-permute-start.6 = (f32[2,2048]{1,0:T(2,128)S(1)}, f32[2,2048]{1,0:T(2,128)S(1)}, u32[]{:S(2)}, u32[]{:S(2)}) collective-permute-start(f32[2,2048]{1,0:T(2,128)S(1)} %copy-done.1), channel_id=1, source_target_pairs={{0,1},{1,0},{2,3},{3,2},{4,5},{5,4},{6,7},{7,6},{8,9},{9,8},{10,11... | collective-permute-start | bytes 49160 | tf_op jit(solution)/shard_map/ppermute | solution.py:43
  23.4 2.7 %collective-permute-done.3 = f32[8,2048]{1,0:T(8,128)S(1)} collective-permute-done((f32[8,2048]{1,0:T(8,128)S(1)}, f32[8,2048]{1,0:T(8,128)S(1)}, u32[]{:S(2)}, u32[]{:S(2)}) %collective-permute-start.3) | collective-permute-done | bytes 65568 | tf_op jit(solution)/shard_map/ppermute | solution.py:43
  26.1 0.8 %collective-permute-start.4 = (f32[4,2048]{1,0:T(4,128)S(1)}, f32[4,2048]{1,0:T(4,128)S(1)}, u32[]{:S(2)}, u32[]{:S(2)}) collective-permute-start(f32[4,2048]{1,0:T(4,128)S(1)} %slice_select_fusion.1), channel_id=1, source_target_pairs={{0,2},{1,3},{2,0},{3,1},{4,6},{5,7},{6,4},{7,5},{8,10},{9,11},{10,... | collective-permute-start | bytes 98312 | tf_op jit(solution)/shard_map/ppermute | solution.py:43
  26.9 2.9 %collective-permute-start.9 = (f32[4,2048]{1,0:T(4,128)S(1)}, f32[4,2048]{1,0:T(4,128)S(1)}, u32[]{:S(2)}, u32[]{:S(2)}) collective-permute-start(f32[4,2048]{1,0:T(4,128)S(1)} %join.1.refs_0_), channel_id=1, source_target_pairs={{0,6},{1,7},{2,4},{3,5},{4,2},{5,3},{6,0},{7,1},{8,14},{9,15},{10,... | collective-permute-start | bytes 98312 | tf_op jit(solution)/shard_map/ppermute | solution.py:43
  29.8 0.6 %collective-permute-start.8 = (f32[4,2048]{1,0:T(4,128)S(1)}, f32[4,2048]{1,0:T(4,128)S(1)}, u32[]{:S(2)}, u32[]{:S(2)}) collective-permute-start(f32[4,2048]{1,0:T(4,128)S(1)} %join.1.refs_0_), channel_id=1, source_target_pairs={{0,4},{1,5},{2,6},{3,7},{4,0},{5,1},{6,2},{7,3},{8,12},{9,13},{10,... | collective-permute-start | bytes 98312 | tf_op jit(solution)/shard_map/ppermute | solution.py:43
  30.4 1.0 %collective-permute-start.7 = (f32[4,2048]{1,0:T(4,128)S(1)}, f32[4,2048]{1,0:T(4,128)S(1)}, u32[]{:S(2)}, u32[]{:S(2)}) collective-permute-start(f32[4,2048]{1,0:T(4,128)S(1)} %join.1.refs_0_), channel_id=1, source_target_pairs={{0,2},{1,3},{2,0},{3,1},{4,6},{5,7},{6,4},{7,5},{8,10},{9,11},{10,... | collective-permute-start | bytes 98312 | tf_op jit(solution)/shard_map/ppermute | solution.py:43
  31.4 0.0 collective-permute-done.4
  31.4 1.6 %collective-permute-start.5 = (f32[2,2048]{1,0:T(2,128)S(1)}, f32[2,2048]{1,0:T(2,128)S(1)}, u32[]{:S(2)}, u32[]{:S(2)}) collective-permute-start(f32[2,2048]{1,0:T(2,128)S(1)} %broadcast_select_fusion), channel_id=1, source_target_pairs={{0,1},{1,0},{2,3},{3,2},{4,5},{5,4},{6,7},{7,6},{8,9},{9,8},{10,11... | collective-permute-start | bytes 49160 | tf_op jit(solution)/shard_map/ppermute | solution.py:43
  33.0 0.0 collective-permute-done.9.refs_3_
  33.0 1.7 %collective-permute-done.8.refs_2_ = f32[4,2048]{1,0:T(4,128)S(1)} collective-permute-done((f32[4,2048]{1,0:T(4,128)S(1)}, f32[4,2048]{1,0:T(4,128)S(1)}, u32[]{:S(2)}, u32[]{:S(2)}) %collective-permute-start.8) | collective-permute-done | bytes 32800 | tf_op jit(solution)/shard_map/ppermute | solution.py:43
  34.7 0.0 collective-permute-done.7.refs_1_
  34.7 4.5 %outer_0.1 = (bf16[48,2048]{1,0:T(8,128)(2,1)S(1)}, f32[2048,3584]{1,0:T(8,128)}) custom-call(f32[4,2048]{1,0:T(4,128)S(1)} %join.1.refs_0_, f32[4,2048]{1,0:T(4,128)S(1)} %collective-permute-done.7.refs_1_, f32[4,2048]{1,0:T(4,128)S(1)} %collective-permute-done.8.refs_2_, f32[4,2048]{1,0:T(4,128)S(1)} %collective-permute-done.9.refs_3_, ...), custom_call_target="tpu_custom_call" | custom-call | tf_op jit(solution)/shard_map/outer_0/pallas_call | solution.py:231
  39.2 3.9 %shard_map.50.begun_ref = f32[2048,3584]{1,0:T(8,128)} custom-call(bf16[48,3584]{1,0:T(8,128)(2,1)S(1)} %get-tuple-element.7.refs_4_.split_ref, bf16[48,2048]{1,0:T(8,128)(2,1)S(1)} %get-tuple-element.8.left_ref, f32[2048,3584]{1,0:T(8,128)} %get-tuple-element.9.begun_ref), custom_call_target="tpu_custom_call", output_to_operand_aliasing={{}: (2, {})} | custom-call | tf_op jit(solution)/shard_map/pallas_call | solution.py:248
  43.2 3.9 %shard_map.51 = f32[2048,3584]{1,0:T(8,128)} custom-call(bf16[48,3584]{1,0:T(8,128)(2,1)S(1)} %get-tuple-element.7.refs_4_.split_ref, bf16[48,2048]{1,0:T(8,128)(2,1)S(1)} %get-tuple-element.8.left_ref, f32[2048,3584]{1,0:T(8,128)} %shard_map.50.begun_ref), custom_call_target="tpu_custom_call", output_to_operand_aliasing={{}: (2, {})} | custom-call | tf_op jit(solution)/shard_map/pallas_call | solution.py:248
  47.1 0.6 %select_add_fusion.2 = f32[2,2048]{1,0:T(2,128)} fusion(f32[2,2048]{1,0:T(2,128)S(1)} %collective-permute-done.5, pred[]{:T(512)S(6)} %eq.13, f32[4,2048]{1,0:T(4,128)S(1)} %select_add_fusion.1), kind=kLoop, calls=%fused_computation.4 | loop fusion | flops 8192 | bytes 65537 | tf_op jit(solution)/shard_map/add | solution.py:291
  (11 shorter events, 0.1 us)
Async XLA Ops:
  0.6 21.2 %copy-start.1 = (f32[2,2048]{1,0:T(2,128)S(1)}, f32[2,2048]{1,0:T(2,128)}, u32[]{:S(2)}) copy-start(f32[2,2048]{1,0:T(2,128)} %own_ref.1) | copy-start | bytes 49156
  0.6 5.5 %collective-permute-start.1 = (f32[4,3584]{1,0:T(4,128)}, f32[4,3584]{1,0:T(4,128)S(1)}, u32[]{:S(2)}, u32[]{:S(2)}) collective-permute-start(f32[4,3584]{1,0:T(4,128)} %refs_0_.1), channel_id=1, source_target_pairs={{0,16},{8,24},{16,0},{24,8},{1,17},{9,25},{17,1},{25,9},{2,18},{10... | collective-permute-start | bytes 172040 | tf_op jit(solution)/shard_map/ppermute | solution.py:43
  3.7 2.5 %collective-permute-start = (f32[4,3584]{1,0:T(4,128)}, f32[4,3584]{1,0:T(4,128)S(1)}, u32[]{:S(2)}, u32[]{:S(2)}) collective-permute-start(f32[4,3584]{1,0:T(4,128)} %refs_0_.1), channel_id=1, source_target_pairs={{0,8},{8,0},{16,24},{24,16},{1,9},{9,1},{17,25},{25,17},{2,10},{10... | collective-permute-start | bytes 172040 | tf_op jit(solution)/shard_map/ppermute | solution.py:43
  3.7 3.8 %collective-permute-start.2 = (f32[4,3584]{1,0:T(4,128)}, f32[4,3584]{1,0:T(4,128)S(1)}, u32[]{:S(2)}, u32[]{:S(2)}) collective-permute-start(f32[4,3584]{1,0:T(4,128)} %refs_0_.1), channel_id=1, source_target_pairs={{0,24},{8,16},{16,8},{24,0},{1,25},{9,17},{17,9},{25,1},{2,26},{10... | collective-permute-start | bytes 172040 | tf_op jit(solution)/shard_map/ppermute | solution.py:43
  7.5 0.8 %copy-start = (f32[4,3584]{1,0:T(4,128)S(1)}, f32[4,3584]{1,0:T(4,128)}, u32[]{:S(2)}) copy-start(f32[4,3584]{1,0:T(4,128)} %refs_0_.1) | copy-start | bytes 172036
  19.2 6.9 %collective-permute-start.3 = (f32[8,2048]{1,0:T(8,128)S(1)}, f32[8,2048]{1,0:T(8,128)S(1)}, u32[]{:S(2)}, u32[]{:S(2)}) collective-permute-start(f32[8,2048]{1,0:T(8,128)S(1)} %slice_select_fusion), channel_id=1, source_target_pairs={{0,4},{1,5},{2,6},{3,7},{4,0},{5,1},{6,2},{7,3},{8,12},{9,13},{10,... | collective-permute-start | bytes 196616 | tf_op jit(solution)/shard_map/ppermute | solution.py:43
  21.9 5.0 %collective-permute-start.6 = (f32[2,2048]{1,0:T(2,128)S(1)}, f32[2,2048]{1,0:T(2,128)S(1)}, u32[]{:S(2)}, u32[]{:S(2)}) collective-permute-start(f32[2,2048]{1,0:T(2,128)S(1)} %copy-done.1), channel_id=1, source_target_pairs={{0,1},{1,0},{2,3},{3,2},{4,5},{5,4},{6,7},{7,6},{8,9},{9,8},{10,11... | collective-permute-start | bytes 49160 | tf_op jit(solution)/shard_map/ppermute | solution.py:43
  26.1 5.2 %collective-permute-start.4 = (f32[4,2048]{1,0:T(4,128)S(1)}, f32[4,2048]{1,0:T(4,128)S(1)}, u32[]{:S(2)}, u32[]{:S(2)}) collective-permute-start(f32[4,2048]{1,0:T(4,128)S(1)} %slice_select_fusion.1), channel_id=1, source_target_pairs={{0,2},{1,3},{2,0},{3,1},{4,6},{5,7},{6,4},{7,5},{8,10},{9,11},{10,... | collective-permute-start | bytes 98312 | tf_op jit(solution)/shard_map/ppermute | solution.py:43
  26.9 6.1 %collective-permute-start.9 = (f32[4,2048]{1,0:T(4,128)S(1)}, f32[4,2048]{1,0:T(4,128)S(1)}, u32[]{:S(2)}, u32[]{:S(2)}) collective-permute-start(f32[4,2048]{1,0:T(4,128)S(1)} %join.1.refs_0_), channel_id=1, source_target_pairs={{0,6},{1,7},{2,4},{3,5},{4,2},{5,3},{6,0},{7,1},{8,14},{9,15},{10,... | collective-permute-start | bytes 98312 | tf_op jit(solution)/shard_map/ppermute | solution.py:43
  29.8 4.9 %collective-permute-start.8 = (f32[4,2048]{1,0:T(4,128)S(1)}, f32[4,2048]{1,0:T(4,128)S(1)}, u32[]{:S(2)}, u32[]{:S(2)}) collective-permute-start(f32[4,2048]{1,0:T(4,128)S(1)} %join.1.refs_0_), channel_id=1, source_target_pairs={{0,4},{1,5},{2,6},{3,7},{4,0},{5,1},{6,2},{7,3},{8,12},{9,13},{10,... | collective-permute-start | bytes 98312 | tf_op jit(solution)/shard_map/ppermute | solution.py:43
  30.4 4.3 %collective-permute-start.7 = (f32[4,2048]{1,0:T(4,128)S(1)}, f32[4,2048]{1,0:T(4,128)S(1)}, u32[]{:S(2)}, u32[]{:S(2)}) collective-permute-start(f32[4,2048]{1,0:T(4,128)S(1)} %join.1.refs_0_), channel_id=1, source_target_pairs={{0,2},{1,3},{2,0},{3,1},{4,6},{5,7},{6,4},{7,5},{8,10},{9,11},{10,... | collective-permute-start | bytes 98312 | tf_op jit(solution)/shard_map/ppermute | solution.py:43
  31.4 15.7 %collective-permute-start.5 = (f32[2,2048]{1,0:T(2,128)S(1)}, f32[2,2048]{1,0:T(2,128)S(1)}, u32[]{:S(2)}, u32[]{:S(2)}) collective-permute-start(f32[2,2048]{1,0:T(2,128)S(1)} %broadcast_select_fusion), channel_id=1, source_target_pairs={{0,1},{1,0},{2,3},{3,2},{4,5},{5,4},{6,7},{7,6},{8,9},{9,8},{10,11... | collective-permute-start | bytes 49160 | tf_op jit(solution)/shard_map/ppermute | solution.py:43

commit v3 on v2

--- a/solution.py
+++ b/solution.py
@@ -18,6 +18,7 @@
 READ_SLOTS = 4
 WRITE_SLOTS = 4
 CUTS = 2
+MARK_FLOPS = 100_000_000_000
 
 
 def plain_body(inputs, out_grad, weight):
@@ -158,7 +159,7 @@
     reader.begin()
     rows = rows_ref.shape[0]
     block = rows // count
-    for position, value in enumerate(in_order(grads, lax.axis_index("din"))):
+    for position, value in enumerate(in_order(grads, lax.axis_index("din") // 2)):
         rows_ref[position * block : (position + 1) * block, :] = value
     high, low = halves(rows_ref[...])
     split_ref[...] = jnp.concatenate([high, low, high], axis=0)
@@ -256,27 +257,45 @@
     )(split, left, buffer)
 
 
-def join_kernel(own_ref, other_ref, out_ref):
+def mark_kernel(out_ref):
+    out_ref[...] = jnp.zeros_like(out_ref)
+
+
+def mark():
+    return pl.pallas_call(
+        mark_kernel,
+        out_shape=pltpu.VMEM((8, 128), F32),
+        out_specs=in_vmem()[0],
+        cost_estimate=pl.CostEstimate(
+            flops=MARK_FLOPS, bytes_accessed=0, transcendentals=0
+        ),
+        compiler_params=pltpu.CompilerParams(vmem_limit_bytes=2 << 20),
+        name="mark",
+    )()
+
+
+def join_kernel(axis, own_ref, other_ref, point_ref, out_ref):
+    del point_ref
     half = own_ref.shape[0]
-    upper = lax.axis_index("dout") % 2
+    upper = lax.axis_index(axis) % 2
     own, other = own_ref[...], other_ref[...]
     out_ref[:half, :] = jnp.where(upper == 1, other, own)
     out_ref[half:, :] = jnp.where(upper == 1, own, other)
 
 
-def join(own, other, cost):
+def join(own, axis, size, point):
     rows, width = own.shape
     return pl.pallas_call(
-        join_kernel,
+        functools.partial(join_kernel, axis),
         out_shape=jax.ShapeDtypeStruct((2 * rows, width), F32),
-        in_specs=in_vmem(2),
+        in_specs=in_vmem(3),
         out_specs=in_vmem()[0],
-        cost_estimate=pl.CostEstimate(
-            flops=cost, bytes_accessed=0, transcendentals=0
-        ),
-        compiler_params=pltpu.CompilerParams(vmem_limit_bytes=2 << 20),
-        name="join",
-    )(own, other)
+        compiler_params=pltpu.CompilerParams(vmem_limit_bytes=4 << 20),
+    )(own, swap(own, axis, size, 1), point)
+
+
+def spread(pair, axis, size):
+    return [pair] + [swap(pair, axis, size, 2 * s) for s in range(1, size // 2)]
 
 
 def bit_of(axis, distance):
@@ -295,10 +314,11 @@
     depth = weight.shape[0]
     rounds = n_out.bit_length() - 1
     weight = pltpu.with_memory_space_constraint(weight, pltpu.MemorySpace.HBM)
-    grads = [out_grad] + [swap(out_grad, "din", n_in, s) for s in range(1, n_in)]
-    pair = join(inputs, swap(inputs, "dout", n_out, 1), 100000000000)
-    pieces = [pair]
-    pieces += [swap(pair, "dout", n_out, 2 * s) for s in range(1, n_out // 2)]
+    point = mark()
+    pair = join(out_grad, "din", n_in, point)
+    grads = spread(pair, "din", n_in)
+    pair = join(inputs, "dout", n_out, point)
+    pieces = spread(pair, "dout", n_out)
     total, split = units(grads, weight, depth // UNITS_TILE, UNITS_TILE)
     first, rest = 0, depth // OUTER_TILE
     for r in range(rounds):
@@ -320,7 +340,7 @@
 def solution(mesh):
     n_in, n_out = mesh.shape["din"], mesh.shape["dout"]
     shaped = (
-        power_of_two(n_in) and power_of_two(n_out) and n_in <= 8 and 4 <= n_out <= 8
+        power_of_two(n_in) and power_of_two(n_out) and 4 <= n_in <= 8 and 4 <= n_out <= 8
     )
 
     def run(inputs, out_grad, weight):

time: 47.9 us -> 51.3 us (1.071)
  waiting for transfers between devices: 8.02 us -> 10.9 us
  starting transfers between devices: 14.2 us -> 15.5 us
  local copies, waits for them, and re-layouts: 0.82 us -> 0.01 us
    ppermute x10 -> x9, waiting for transfers between devices: 8.02 us -> 10.9 us  [swap(): return lax.ppermute(value, axis, [(i, i ^ distance) for i in range(size)])]
    ppermute x10 -> x9, starting transfers between devices: 14.2 us -> 15.5 us  [swap(): return lax.ppermute(value, axis, [(i, i ^ distance) for i in range(size)])]
    unnamed x4, local copies, waits for them, and re-layouts: 0.82 us -> 0.01 us
  transfers between devices with their start and end apart: 10 -> 9, of which waited for: 4 -> 5; matrix products, arithmetic and copies ran while one was open for 0% -> 0% of each run, Pallas kernels for 26% -> 24%
where the time goes in v3:
time: 51.3 us; the launch traced here: 51.2 us
  Pallas kernels  23.3 us (45%)
  starting transfers between devices  15.5 us (30%)
  waiting for transfers between devices  10.9 us (21%)
  between operations  0.73 us (1%)
  other arithmetic  0.68 us (1%)
    ppermute x9, starting transfers between devices, swap(): return lax.ppermute(value, axis, [(i, i ^ distance) for i in range(size)])  15.5 us
    ppermute x9, waiting for transfers between devices, swap(): return lax.ppermute(value, axis, [(i, i ^ distance) for i in range(size)])  10.9 us
    pallas_call x1, Pallas kernels, units(): pl.pallas_call(functools.partial(units_kernel, count, steps), out_shape=[...  10.9 us
    pallas_call x2, Pallas kernels, outer(): pl.pallas_call(functools.partial(later_kernel, first, steps), out_shape=j...  7.89 us
    pallas_call x1, Pallas kernels, outer_first(): pl.pallas_call(functools.partial(outer_kernel, count, 0, steps), out_shap...  4.55 us
  transfers between devices with their start and end apart: 9, of which 5 were waited for; matrix products, arithmetic and copies ran while one was open for 0% of the time, Pallas kernels for 24%

profile of v3, /device:TPU:0, one launch (start us, length us, event | category | flops | bytes accessed | tf_op | source)
XLA Modules:
  0.0 51.2 jit_solution(10548714252128017447)
XLA Ops:
  0.6 0.0 copy-start
  0.6 0.6 %collective-permute-start = (f32[4,3584]{1,0:T(4,128)}, f32[4,3584]{1,0:T(4,128)S(1)}, u32[]{:S(2)}, u32[]{:S(2)}) collective-permute-start(f32[4,3584]{1,0:T(4,128)} %own_ref.2), channel_id=1, source_target_pairs={{0,8},{8,0},{16,24},{24,16},{1,9},{9,1},{17,25},{25,17},{2,10},{10... | collective-permute-start | bytes 172040 | tf_op jit(solution)/shard_map/ppermute | solution.py:44
  1.2 1.1 %collective-permute-done.other_ref = f32[4,3584]{1,0:T(4,128)S(1)} collective-permute-done((f32[4,3584]{1,0:T(4,128)}, f32[4,3584]{1,0:T(4,128)S(1)}, u32[]{:S(2)}, u32[]{:S(2)}) %collective-permute-start) | collective-permute-done | bytes 57376 | tf_op jit(solution)/shard_map/ppermute | solution.py:44
  2.3 2.9 %collective-permute-start.1 = (f32[8,3584]{1,0:T(8,128)S(1)}, f32[8,3584]{1,0:T(8,128)S(1)}, u32[]{:S(2)}, u32[]{:S(2)}) collective-permute-start(f32[8,3584]{1,0:T(8,128)S(1)} %shard_map.50.refs_0_), channel_id=1, source_target_pairs={{0,16},{8,24},{16,0},{24,8},{1,17},{9,25},{17,1},{25,9},{2,18},{10... | collective-permute-start | bytes 344072 | tf_op jit(solution)/shard_map/ppermute | solution.py:44
  5.2 3.5 %collective-permute-done.1.refs_1_ = f32[8,3584]{1,0:T(8,128)S(1)} collective-permute-done((f32[8,3584]{1,0:T(8,128)S(1)}, f32[8,3584]{1,0:T(8,128)S(1)}, u32[]{:S(2)}, u32[]{:S(2)}) %collective-permute-start.1) | collective-permute-done | bytes 114720 | tf_op jit(solution)/shard_map/ppermute | solution.py:44
  8.7 10.9 %units.1 = (f32[16,2048]{1,0:T(8,128)S(1)}, bf16[48,3584]{1,0:T(8,128)(2,1)S(1)}) custom-call(f32[8,3584]{1,0:T(8,128)S(1)} %shard_map.50.refs_0_, f32[8,3584]{1,0:T(8,128)S(1)} %collective-permute-done.1.refs_1_, f32[2048,3584]{1,0:T(8,128)} %refs_2_.1), custom_call_target="tpu_custom_call" | custom-call | tf_op jit(solution)/shard_map/units/pallas_call | solution.py:194
  19.6 2.9 %collective-permute-start.2 = (f32[8,2048]{1,0:T(8,128)S(1)}, f32[8,2048]{1,0:T(8,128)S(1)}, u32[]{:S(2)}, u32[]{:S(2)}) collective-permute-start(f32[8,2048]{1,0:T(8,128)S(1)} %slice_select_fusion), channel_id=1, source_target_pairs={{0,4},{1,5},{2,6},{3,7},{4,0},{5,1},{6,2},{7,3},{8,12},{9,13},{10,... | collective-permute-start | bytes 196616 | tf_op jit(solution)/shard_map/ppermute | solution.py:44
  22.5 2.6 %collective-permute-done.2 = f32[8,2048]{1,0:T(8,128)S(1)} collective-permute-done((f32[8,2048]{1,0:T(8,128)S(1)}, f32[8,2048]{1,0:T(8,128)S(1)}, u32[]{:S(2)}, u32[]{:S(2)}) %collective-permute-start.2) | collective-permute-done | bytes 65568 | tf_op jit(solution)/shard_map/ppermute | solution.py:44
  25.1 1.6 %collective-permute-start.3 = (f32[4,2048]{1,0:T(4,128)S(1)}, f32[4,2048]{1,0:T(4,128)S(1)}, u32[]{:S(2)}, u32[]{:S(2)}) collective-permute-start(f32[4,2048]{1,0:T(4,128)S(1)} %slice_select_fusion.1), channel_id=1, source_target_pairs={{0,2},{1,3},{2,0},{3,1},{4,6},{5,7},{6,4},{7,5},{8,10},{9,11},{10,... | collective-permute-start | bytes 98312 | tf_op jit(solution)/shard_map/ppermute | solution.py:44
  26.7 1.5 %collective-permute-start.5 = (f32[2,2048]{1,0:T(2,128)S(1)}, f32[2,2048]{1,0:T(2,128)S(1)}, u32[]{:S(2)}, u32[]{:S(2)}) collective-permute-start(f32[2,2048]{1,0:T(2,128)S(1)} %copy-done.1), channel_id=1, source_target_pairs={{0,1},{1,0},{2,3},{3,2},{4,5},{5,4},{6,7},{7,6},{8,9},{9,8},{10,11... | collective-permute-start | bytes 49160 | tf_op jit(solution)/shard_map/ppermute | solution.py:44
  28.3 2.2 %collective-permute-done.5.other_ref = f32[2,2048]{1,0:T(2,128)S(1)} collective-permute-done((f32[2,2048]{1,0:T(2,128)S(1)}, f32[2,2048]{1,0:T(2,128)S(1)}, u32[]{:S(2)}, u32[]{:S(2)}) %collective-permute-start.5) | collective-permute-done | bytes 16416 | tf_op jit(solution)/shard_map/ppermute | solution.py:44
  30.5 2.8 %collective-permute-start.8 = (f32[4,2048]{1,0:T(4,128)S(1)}, f32[4,2048]{1,0:T(4,128)S(1)}, u32[]{:S(2)}, u32[]{:S(2)}) collective-permute-start(f32[4,2048]{1,0:T(4,128)S(1)} %shard_map.51.refs_0_), channel_id=1, source_target_pairs={{0,6},{1,7},{2,4},{3,5},{4,2},{5,3},{6,0},{7,1},{8,14},{9,15},{10,... | collective-permute-start | bytes 98312 | tf_op jit(solution)/shard_map/ppermute | solution.py:44
  33.3 0.6 %collective-permute-start.7 = (f32[4,2048]{1,0:T(4,128)S(1)}, f32[4,2048]{1,0:T(4,128)S(1)}, u32[]{:S(2)}, u32[]{:S(2)}) collective-permute-start(f32[4,2048]{1,0:T(4,128)S(1)} %shard_map.51.refs_0_), channel_id=1, source_target_pairs={{0,4},{1,5},{2,6},{3,7},{4,0},{5,1},{6,2},{7,3},{8,12},{9,13},{10,... | collective-permute-start | bytes 98312 | tf_op jit(solution)/shard_map/ppermute | solution.py:44
  33.8 1.1 %collective-permute-start.6 = (f32[4,2048]{1,0:T(4,128)S(1)}, f32[4,2048]{1,0:T(4,128)S(1)}, u32[]{:S(2)}, u32[]{:S(2)}) collective-permute-start(f32[4,2048]{1,0:T(4,128)S(1)} %shard_map.51.refs_0_), channel_id=1, source_target_pairs={{0,2},{1,3},{2,0},{3,1},{4,6},{5,7},{6,4},{7,5},{8,10},{9,11},{10,... | collective-permute-start | bytes 98312 | tf_op jit(solution)/shard_map/ppermute | solution.py:44
  35.0 0.0 collective-permute-done.3
  35.0 1.6 %collective-permute-start.4 = (f32[2,2048]{1,0:T(2,128)S(1)}, f32[2,2048]{1,0:T(2,128)S(1)}, u32[]{:S(2)}, u32[]{:S(2)}) collective-permute-start(f32[2,2048]{1,0:T(2,128)S(1)} %broadcast_select_fusion), channel_id=1, source_target_pairs={{0,1},{1,0},{2,3},{3,2},{4,5},{5,4},{6,7},{7,6},{8,9},{9,8},{10,11... | collective-permute-start | bytes 49160 | tf_op jit(solution)/shard_map/ppermute | solution.py:44
  36.6 0.0 collective-permute-done.8.refs_3_
  36.6 1.5 %collective-permute-done.7.refs_2_ = f32[4,2048]{1,0:T(4,128)S(1)} collective-permute-done((f32[4,2048]{1,0:T(4,128)S(1)}, f32[4,2048]{1,0:T(4,128)S(1)}, u32[]{:S(2)}, u32[]{:S(2)}) %collective-permute-start.7) | collective-permute-done | bytes 32800 | tf_op jit(solution)/shard_map/ppermute | solution.py:44
  38.1 0.0 collective-permute-done.6.refs_1_
  38.1 4.5 %outer_0.1 = (bf16[48,2048]{1,0:T(8,128)(2,1)S(1)}, f32[2048,3584]{1,0:T(8,128)}) custom-call(f32[4,2048]{1,0:T(4,128)S(1)} %shard_map.51.refs_0_, f32[4,2048]{1,0:T(4,128)S(1)} %collective-permute-done.6.refs_1_, f32[4,2048]{1,0:T(4,128)S(1)} %collective-permute-done.7.refs_2_, f32[4,2048]{1,0:T(4,128)S(1)} %collective-permute-done.8.refs_3_, ...), custom_call_target="tpu_custom_call" | custom-call | tf_op jit(solution)/shard_map/outer_0/pallas_call | solution.py:232
  42.6 3.9 %shard_map.52.begun_ref = f32[2048,3584]{1,0:T(8,128)} custom-call(bf16[48,3584]{1,0:T(8,128)(2,1)S(1)} %get-tuple-element.7.refs_4_.split_ref, bf16[48,2048]{1,0:T(8,128)(2,1)S(1)} %get-tuple-element.8.left_ref, f32[2048,3584]{1,0:T(8,128)} %get-tuple-element.9.begun_ref), custom_call_target="tpu_custom_call", output_to_operand_aliasing={{}: (2, {})} | custom-call | tf_op jit(solution)/shard_map/pallas_call | solution.py:249
  46.6 4.0 %shard_map.53 = f32[2048,3584]{1,0:T(8,128)} custom-call(bf16[48,3584]{1,0:T(8,128)(2,1)S(1)} %get-tuple-element.7.refs_4_.split_ref, bf16[48,2048]{1,0:T(8,128)(2,1)S(1)} %get-tuple-element.8.left_ref, f32[2048,3584]{1,0:T(8,128)} %shard_map.52.begun_ref), custom_call_target="tpu_custom_call", output_to_operand_aliasing={{}: (2, {})} | custom-call | tf_op jit(solution)/shard_map/pallas_call | solution.py:249
  50.6 0.0 collective-permute-done.4
  50.6 0.6 %select_add_fusion.2 = f32[2,2048]{1,0:T(2,128)} fusion(f32[2,2048]{1,0:T(2,128)S(1)} %collective-permute-done.4, pred[]{:T(512)S(6)} %eq.13, f32[4,2048]{1,0:T(4,128)S(1)} %select_add_fusion.1), kind=kLoop, calls=%fused_computation.4 | loop fusion | flops 8192 | bytes 65537 | tf_op jit(solution)/shard_map/add | solution.py:310
  (11 shorter events, 0.1 us)
Async XLA Ops:
  0.6 1.7 %copy-start = (f32[4,3584]{1,0:T(4,128)S(1)}, f32[4,3584]{1,0:T(4,128)}, u32[]{:S(2)}) copy-start(f32[4,3584]{1,0:T(4,128)} %own_ref.2) | copy-start | bytes 172036
  0.6 1.7 %collective-permute-start = (f32[4,3584]{1,0:T(4,128)}, f32[4,3584]{1,0:T(4,128)S(1)}, u32[]{:S(2)}, u32[]{:S(2)}) collective-permute-start(f32[4,3584]{1,0:T(4,128)} %own_ref.2), channel_id=1, source_target_pairs={{0,8},{8,0},{16,24},{24,16},{1,9},{9,1},{17,25},{25,17},{2,10},{10... | collective-permute-start | bytes 172040 | tf_op jit(solution)/shard_map/ppermute | solution.py:44
  1.2 25.5 %copy-start.1 = (f32[2,2048]{1,0:T(2,128)S(1)}, f32[2,2048]{1,0:T(2,128)}, u32[]{:S(2)}) copy-start(f32[2,2048]{1,0:T(2,128)} %own_ref.3) | copy-start | bytes 49156
  2.3 6.4 %collective-permute-start.1 = (f32[8,3584]{1,0:T(8,128)S(1)}, f32[8,3584]{1,0:T(8,128)S(1)}, u32[]{:S(2)}, u32[]{:S(2)}) collective-permute-start(f32[8,3584]{1,0:T(8,128)S(1)} %shard_map.50.refs_0_), channel_id=1, source_target_pairs={{0,16},{8,24},{16,0},{24,8},{1,17},{9,25},{17,1},{25,9},{2,18},{10... | collective-permute-start | bytes 344072 | tf_op jit(solution)/shard_map/ppermute | solution.py:44
  19.6 5.5 %collective-permute-start.2 = (f32[8,2048]{1,0:T(8,128)S(1)}, f32[8,2048]{1,0:T(8,128)S(1)}, u32[]{:S(2)}, u32[]{:S(2)}) collective-permute-start(f32[8,2048]{1,0:T(8,128)S(1)} %slice_select_fusion), channel_id=1, source_target_pairs={{0,4},{1,5},{2,6},{3,7},{4,0},{5,1},{6,2},{7,3},{8,12},{9,13},{10,... | collective-permute-start | bytes 196616 | tf_op jit(solution)/shard_map/ppermute | solution.py:44
  25.1 9.8 %collective-permute-start.3 = (f32[4,2048]{1,0:T(4,128)S(1)}, f32[4,2048]{1,0:T(4,128)S(1)}, u32[]{:S(2)}, u32[]{:S(2)}) collective-permute-start(f32[4,2048]{1,0:T(4,128)S(1)} %slice_select_fusion.1), channel_id=1, source_target_pairs={{0,2},{1,3},{2,0},{3,1},{4,6},{5,7},{6,4},{7,5},{8,10},{9,11},{10,... | collective-permute-start | bytes 98312 | tf_op jit(solution)/shard_map/ppermute | solution.py:44
  26.7 3.7 %collective-permute-start.5 = (f32[2,2048]{1,0:T(2,128)S(1)}, f32[2,2048]{1,0:T(2,128)S(1)}, u32[]{:S(2)}, u32[]{:S(2)}) collective-permute-start(f32[2,2048]{1,0:T(2,128)S(1)} %copy-done.1), channel_id=1, source_target_pairs={{0,1},{1,0},{2,3},{3,2},{4,5},{5,4},{6,7},{7,6},{8,9},{9,8},{10,11... | collective-permute-start | bytes 49160 | tf_op jit(solution)/shard_map/ppermute | solution.py:44
  30.5 6.1 %collective-permute-start.8 = (f32[4,2048]{1,0:T(4,128)S(1)}, f32[4,2048]{1,0:T(4,128)S(1)}, u32[]{:S(2)}, u32[]{:S(2)}) collective-permute-start(f32[4,2048]{1,0:T(4,128)S(1)} %shard_map.51.refs_0_), channel_id=1, source_target_pairs={{0,6},{1,7},{2,4},{3,5},{4,2},{5,3},{6,0},{7,1},{8,14},{9,15},{10,... | collective-permute-start | bytes 98312 | tf_op jit(solution)/shard_map/ppermute | solution.py:44
  33.3 4.8 %collective-permute-start.7 = (f32[4,2048]{1,0:T(4,128)S(1)}, f32[4,2048]{1,0:T(4,128)S(1)}, u32[]{:S(2)}, u32[]{:S(2)}) collective-permute-start(f32[4,2048]{1,0:T(4,128)S(1)} %shard_map.51.refs_0_), channel_id=1, source_target_pairs={{0,4},{1,5},{2,6},{3,7},{4,0},{5,1},{6,2},{7,3},{8,12},{9,13},{10,... | collective-permute-start | bytes 98312 | tf_op jit(solution)/shard_map/ppermute | solution.py:44
  33.8 4.3 %collective-permute-start.6 = (f32[4,2048]{1,0:T(4,128)S(1)}, f32[4,2048]{1,0:T(4,128)S(1)}, u32[]{:S(2)}, u32[]{:S(2)}) collective-permute-start(f32[4,2048]{1,0:T(4,128)S(1)} %shard_map.51.refs_0_), channel_id=1, source_target_pairs={{0,2},{1,3},{2,0},{3,1},{4,6},{5,7},{6,4},{7,5},{8,10},{9,11},{10,... | collective-permute-start | bytes 98312 | tf_op jit(solution)/shard_map/ppermute | solution.py:44
  35.0 15.6 %collective-permute-start.4 = (f32[2,2048]{1,0:T(2,128)S(1)}, f32[2,2048]{1,0:T(2,128)S(1)}, u32[]{:S(2)}, u32[]{:S(2)}) collective-permute-start(f32[2,2048]{1,0:T(2,128)S(1)} %broadcast_select_fusion), channel_id=1, source_target_pairs={{0,1},{1,0},{2,3},{3,2},{4,5},{5,4},{6,7},{7,6},{8,9},{9,8},{10,11... | collective-permute-start | bytes 49160 | tf_op jit(solution)/shard_map/ppermute | solution.py:44

commit v4 on v3

--- a/solution.py
+++ b/solution.py
@@ -15,7 +15,7 @@
 
 UNITS_TILE = 256
 OUTER_TILE = 128
-READ_SLOTS = 4
+READ_SLOTS = 6
 WRITE_SLOTS = 4
 CUTS = 2
 MARK_FLOPS = 100_000_000_000
@@ -81,8 +81,8 @@
             self.sems.at[slot],
         )
 
-    def begin(self):
-        for step in range(self.ahead):
+    def begin(self, first, last):
+        for step in range(first, min(last, self.ahead)):
             self.copy(step).start()
 
     def arrive(self, step):
@@ -156,13 +156,14 @@
     grads, refs = refs[:count], refs[count:]
     w_ref, out_ref, split_ref, rows_ref, slots, sems = refs
     reader = Reader(w_ref, slots, sems, 0, steps)
-    reader.begin()
+    reader.begin(0, 1)
     rows = rows_ref.shape[0]
     block = rows // count
     for position, value in enumerate(in_order(grads, lax.axis_index("din") // 2)):
         rows_ref[position * block : (position + 1) * block, :] = value
     high, low = halves(rows_ref[...])
     split_ref[...] = jnp.concatenate([high, low, high], axis=0)
+    reader.begin(1, READ_SLOTS)
 
     def run(step):
         tile = slots.shape[1]

time: 51.3 us -> 51.3 us (level)
  no operation moved by 1% of the time
where the time goes in v4:
time: 51.3 us; the launch traced here: 51.1 us
  Pallas kernels  23.3 us (45%)
  starting transfers between devices  15.5 us (30%)
  waiting for transfers between devices  10.9 us (21%)
  between operations  0.73 us (1%)
  other arithmetic  0.68 us (1%)
    ppermute x9, starting transfers between devices, swap(): return lax.ppermute(value, axis, [(i, i ^ distance) for i in range(size)])  15.5 us
    ppermute x9, waiting for transfers between devices, swap(): return lax.ppermute(value, axis, [(i, i ^ distance) for i in range(size)])  10.9 us
    pallas_call x1, Pallas kernels, units(): pl.pallas_call(functools.partial(units_kernel, count, steps), out_shape=[...  10.8 us
    pallas_call x2, Pallas kernels, outer(): pl.pallas_call(functools.partial(later_kernel, first, steps), out_shape=j...  7.89 us
    pallas_call x1, Pallas kernels, outer_first(): pl.pallas_call(functools.partial(outer_kernel, count, 0, steps), out_shap...  4.54 us
  transfers between devices with their start and end apart: 9, of which 5 were waited for; matrix products, arithmetic and copies ran while one was open for 0% of the time, Pallas kernels for 24%

profile of v4, /device:TPU:0, one launch (start us, length us, event | category | flops | bytes accessed | tf_op | source)
XLA Modules:
  0.0 51.1 jit_solution(1397238746123709081)
XLA Ops:
  0.6 0.6 %collective-permute-start = (f32[4,3584]{1,0:T(4,128)}, f32[4,3584]{1,0:T(4,128)S(1)}, u32[]{:S(2)}, u32[]{:S(2)}) collective-permute-start(f32[4,3584]{1,0:T(4,128)} %own_ref.2), channel_id=1, source_target_pairs={{0,8},{8,0},{16,24},{24,16},{1,9},{9,1},{17,25},{25,17},{2,10},{10... | collective-permute-start | bytes 172040 | tf_op jit(solution)/shard_map/ppermute | solution.py:44
  1.2 1.1 %collective-permute-done.other_ref = f32[4,3584]{1,0:T(4,128)S(1)} collective-permute-done((f32[4,3584]{1,0:T(4,128)}, f32[4,3584]{1,0:T(4,128)S(1)}, u32[]{:S(2)}, u32[]{:S(2)}) %collective-permute-start) | collective-permute-done | bytes 57376 | tf_op jit(solution)/shard_map/ppermute | solution.py:44
  2.3 2.9 %collective-permute-start.1 = (f32[8,3584]{1,0:T(8,128)S(1)}, f32[8,3584]{1,0:T(8,128)S(1)}, u32[]{:S(2)}, u32[]{:S(2)}) collective-permute-start(f32[8,3584]{1,0:T(8,128)S(1)} %shard_map.50.refs_0_), channel_id=1, source_target_pairs={{0,16},{8,24},{16,0},{24,8},{1,17},{9,25},{17,1},{25,9},{2,18},{10... | collective-permute-start | bytes 344072 | tf_op jit(solution)/shard_map/ppermute | solution.py:44
  5.2 3.5 %collective-permute-done.1.refs_1_ = f32[8,3584]{1,0:T(8,128)S(1)} collective-permute-done((f32[8,3584]{1,0:T(8,128)S(1)}, f32[8,3584]{1,0:T(8,128)S(1)}, u32[]{:S(2)}, u32[]{:S(2)}) %collective-permute-start.1) | collective-permute-done | bytes 114720 | tf_op jit(solution)/shard_map/ppermute | solution.py:44
  8.7 10.8 %units.1 = (f32[16,2048]{1,0:T(8,128)S(1)}, bf16[48,3584]{1,0:T(8,128)(2,1)S(1)}) custom-call(f32[8,3584]{1,0:T(8,128)S(1)} %shard_map.50.refs_0_, f32[8,3584]{1,0:T(8,128)S(1)} %collective-permute-done.1.refs_1_, f32[2048,3584]{1,0:T(8,128)} %refs_2_.1), custom_call_target="tpu_custom_call" | custom-call | tf_op jit(solution)/shard_map/units/pallas_call | solution.py:195
  19.5 2.9 %collective-permute-start.2 = (f32[8,2048]{1,0:T(8,128)S(1)}, f32[8,2048]{1,0:T(8,128)S(1)}, u32[]{:S(2)}, u32[]{:S(2)}) collective-permute-start(f32[8,2048]{1,0:T(8,128)S(1)} %slice_select_fusion), channel_id=1, source_target_pairs={{0,4},{1,5},{2,6},{3,7},{4,0},{5,1},{6,2},{7,3},{8,12},{9,13},{10,... | collective-permute-start | bytes 196616 | tf_op jit(solution)/shard_map/ppermute | solution.py:44
  22.4 2.6 %collective-permute-done.2 = f32[8,2048]{1,0:T(8,128)S(1)} collective-permute-done((f32[8,2048]{1,0:T(8,128)S(1)}, f32[8,2048]{1,0:T(8,128)S(1)}, u32[]{:S(2)}, u32[]{:S(2)}) %collective-permute-start.2) | collective-permute-done | bytes 65568 | tf_op jit(solution)/shard_map/ppermute | solution.py:44
  25.1 1.6 %collective-permute-start.3 = (f32[4,2048]{1,0:T(4,128)S(1)}, f32[4,2048]{1,0:T(4,128)S(1)}, u32[]{:S(2)}, u32[]{:S(2)}) collective-permute-start(f32[4,2048]{1,0:T(4,128)S(1)} %slice_select_fusion.1), channel_id=1, source_target_pairs={{0,2},{1,3},{2,0},{3,1},{4,6},{5,7},{6,4},{7,5},{8,10},{9,11},{10,... | collective-permute-start | bytes 98312 | tf_op jit(solution)/shard_map/ppermute | solution.py:44
  26.7 0.0 copy-done.1
  26.7 1.5 %collective-permute-start.5 = (f32[2,2048]{1,0:T(2,128)S(1)}, f32[2,2048]{1,0:T(2,128)S(1)}, u32[]{:S(2)}, u32[]{:S(2)}) collective-permute-start(f32[2,2048]{1,0:T(2,128)S(1)} %copy-done.1), channel_id=1, source_target_pairs={{0,1},{1,0},{2,3},{3,2},{4,5},{5,4},{6,7},{7,6},{8,9},{9,8},{10,11... | collective-permute-start | bytes 49160 | tf_op jit(solution)/shard_map/ppermute | solution.py:44
  28.2 2.2 %collective-permute-done.5.other_ref = f32[2,2048]{1,0:T(2,128)S(1)} collective-permute-done((f32[2,2048]{1,0:T(2,128)S(1)}, f32[2,2048]{1,0:T(2,128)S(1)}, u32[]{:S(2)}, u32[]{:S(2)}) %collective-permute-start.5) | collective-permute-done | bytes 16416 | tf_op jit(solution)/shard_map/ppermute | solution.py:44
  30.5 2.8 %collective-permute-start.8 = (f32[4,2048]{1,0:T(4,128)S(1)}, f32[4,2048]{1,0:T(4,128)S(1)}, u32[]{:S(2)}, u32[]{:S(2)}) collective-permute-start(f32[4,2048]{1,0:T(4,128)S(1)} %shard_map.51.refs_0_), channel_id=1, source_target_pairs={{0,6},{1,7},{2,4},{3,5},{4,2},{5,3},{6,0},{7,1},{8,14},{9,15},{10,... | collective-permute-start | bytes 98312 | tf_op jit(solution)/shard_map/ppermute | solution.py:44
  33.2 0.6 %collective-permute-start.7 = (f32[4,2048]{1,0:T(4,128)S(1)}, f32[4,2048]{1,0:T(4,128)S(1)}, u32[]{:S(2)}, u32[]{:S(2)}) collective-permute-start(f32[4,2048]{1,0:T(4,128)S(1)} %shard_map.51.refs_0_), channel_id=1, source_target_pairs={{0,4},{1,5},{2,6},{3,7},{4,0},{5,1},{6,2},{7,3},{8,12},{9,13},{10,... | collective-permute-start | bytes 98312 | tf_op jit(solution)/shard_map/ppermute | solution.py:44
  33.8 1.1 %collective-permute-start.6 = (f32[4,2048]{1,0:T(4,128)S(1)}, f32[4,2048]{1,0:T(4,128)S(1)}, u32[]{:S(2)}, u32[]{:S(2)}) collective-permute-start(f32[4,2048]{1,0:T(4,128)S(1)} %shard_map.51.refs_0_), channel_id=1, source_target_pairs={{0,2},{1,3},{2,0},{3,1},{4,6},{5,7},{6,4},{7,5},{8,10},{9,11},{10,... | collective-permute-start | bytes 98312 | tf_op jit(solution)/shard_map/ppermute | solution.py:44
  34.9 0.0 collective-permute-done.3
  34.9 1.6 %collective-permute-start.4 = (f32[2,2048]{1,0:T(2,128)S(1)}, f32[2,2048]{1,0:T(2,128)S(1)}, u32[]{:S(2)}, u32[]{:S(2)}) collective-permute-start(f32[2,2048]{1,0:T(2,128)S(1)} %broadcast_select_fusion), channel_id=1, source_target_pairs={{0,1},{1,0},{2,3},{3,2},{4,5},{5,4},{6,7},{7,6},{8,9},{9,8},{10,11... | collective-permute-start | bytes 49160 | tf_op jit(solution)/shard_map/ppermute | solution.py:44
  36.5 0.0 collective-permute-done.8.refs_3_
  36.5 1.5 %collective-permute-done.7.refs_2_ = f32[4,2048]{1,0:T(4,128)S(1)} collective-permute-done((f32[4,2048]{1,0:T(4,128)S(1)}, f32[4,2048]{1,0:T(4,128)S(1)}, u32[]{:S(2)}, u32[]{:S(2)}) %collective-permute-start.7) | collective-permute-done | bytes 32800 | tf_op jit(solution)/shard_map/ppermute | solution.py:44
  38.0 0.0 collective-permute-done.6.refs_1_
  38.0 4.5 %outer_0.1 = (bf16[48,2048]{1,0:T(8,128)(2,1)S(1)}, f32[2048,3584]{1,0:T(8,128)}) custom-call(f32[4,2048]{1,0:T(4,128)S(1)} %shard_map.51.refs_0_, f32[4,2048]{1,0:T(4,128)S(1)} %collective-permute-done.6.refs_1_, f32[4,2048]{1,0:T(4,128)S(1)} %collective-permute-done.7.refs_2_, f32[4,2048]{1,0:T(4,128)S(1)} %collective-permute-done.8.refs_3_, ...), custom_call_target="tpu_custom_call" | custom-call | tf_op jit(solution)/shard_map/outer_0/pallas_call | solution.py:233
  42.6 3.9 %shard_map.52.begun_ref = f32[2048,3584]{1,0:T(8,128)} custom-call(bf16[48,3584]{1,0:T(8,128)(2,1)S(1)} %get-tuple-element.7.refs_4_.split_ref, bf16[48,2048]{1,0:T(8,128)(2,1)S(1)} %get-tuple-element.8.left_ref, f32[2048,3584]{1,0:T(8,128)} %get-tuple-element.9.begun_ref), custom_call_target="tpu_custom_call", output_to_operand_aliasing={{}: (2, {})} | custom-call | tf_op jit(solution)/shard_map/pallas_call | solution.py:250
  46.5 4.0 %shard_map.53 = f32[2048,3584]{1,0:T(8,128)} custom-call(bf16[48,3584]{1,0:T(8,128)(2,1)S(1)} %get-tuple-element.7.refs_4_.split_ref, bf16[48,2048]{1,0:T(8,128)(2,1)S(1)} %get-tuple-element.8.left_ref, f32[2048,3584]{1,0:T(8,128)} %shard_map.52.begun_ref), custom_call_target="tpu_custom_call", output_to_operand_aliasing={{}: (2, {})} | custom-call | tf_op jit(solution)/shard_map/pallas_call | solution.py:250
  50.5 0.0 collective-permute-done.4
  50.5 0.6 %select_add_fusion.2 = f32[2,2048]{1,0:T(2,128)} fusion(f32[2,2048]{1,0:T(2,128)S(1)} %collective-permute-done.4, pred[]{:T(512)S(6)} %eq.13, f32[4,2048]{1,0:T(4,128)S(1)} %select_add_fusion.1), kind=kLoop, calls=%fused_computation.4 | loop fusion | flops 8192 | bytes 65537 | tf_op jit(solution)/shard_map/add | solution.py:311
  (11 shorter events, 0.1 us)
Async XLA Ops:
  0.6 1.7 %copy-start = (f32[4,3584]{1,0:T(4,128)S(1)}, f32[4,3584]{1,0:T(4,128)}, u32[]{:S(2)}) copy-start(f32[4,3584]{1,0:T(4,128)} %own_ref.2) | copy-start | bytes 172036
  0.6 1.7 %collective-permute-start = (f32[4,3584]{1,0:T(4,128)}, f32[4,3584]{1,0:T(4,128)S(1)}, u32[]{:S(2)}, u32[]{:S(2)}) collective-permute-start(f32[4,3584]{1,0:T(4,128)} %own_ref.2), channel_id=1, source_target_pairs={{0,8},{8,0},{16,24},{24,16},{1,9},{9,1},{17,25},{25,17},{2,10},{10... | collective-permute-start | bytes 172040 | tf_op jit(solution)/shard_map/ppermute | solution.py:44
  1.2 25.5 %copy-start.1 = (f32[2,2048]{1,0:T(2,128)S(1)}, f32[2,2048]{1,0:T(2,128)}, u32[]{:S(2)}) copy-start(f32[2,2048]{1,0:T(2,128)} %own_ref.3) | copy-start | bytes 49156
  2.3 6.4 %collective-permute-start.1 = (f32[8,3584]{1,0:T(8,128)S(1)}, f32[8,3584]{1,0:T(8,128)S(1)}, u32[]{:S(2)}, u32[]{:S(2)}) collective-permute-start(f32[8,3584]{1,0:T(8,128)S(1)} %shard_map.50.refs_0_), channel_id=1, source_target_pairs={{0,16},{8,24},{16,0},{24,8},{1,17},{9,25},{17,1},{25,9},{2,18},{10... | collective-permute-start | bytes 344072 | tf_op jit(solution)/shard_map/ppermute | solution.py:44
  19.5 5.5 %collective-permute-start.2 = (f32[8,2048]{1,0:T(8,128)S(1)}, f32[8,2048]{1,0:T(8,128)S(1)}, u32[]{:S(2)}, u32[]{:S(2)}) collective-permute-start(f32[8,2048]{1,0:T(8,128)S(1)} %slice_select_fusion), channel_id=1, source_target_pairs={{0,4},{1,5},{2,6},{3,7},{4,0},{5,1},{6,2},{7,3},{8,12},{9,13},{10,... | collective-permute-start | bytes 196616 | tf_op jit(solution)/shard_map/ppermute | solution.py:44
  25.1 9.8 %collective-permute-start.3 = (f32[4,2048]{1,0:T(4,128)S(1)}, f32[4,2048]{1,0:T(4,128)S(1)}, u32[]{:S(2)}, u32[]{:S(2)}) collective-permute-start(f32[4,2048]{1,0:T(4,128)S(1)} %slice_select_fusion.1), channel_id=1, source_target_pairs={{0,2},{1,3},{2,0},{3,1},{4,6},{5,7},{6,4},{7,5},{8,10},{9,11},{10,... | collective-permute-start | bytes 98312 | tf_op jit(solution)/shard_map/ppermute | solution.py:44
  26.7 3.7 %collective-permute-start.5 = (f32[2,2048]{1,0:T(2,128)S(1)}, f32[2,2048]{1,0:T(2,128)S(1)}, u32[]{:S(2)}, u32[]{:S(2)}) collective-permute-start(f32[2,2048]{1,0:T(2,128)S(1)} %copy-done.1), channel_id=1, source_target_pairs={{0,1},{1,0},{2,3},{3,2},{4,5},{5,4},{6,7},{7,6},{8,9},{9,8},{10,11... | collective-permute-start | bytes 49160 | tf_op jit(solution)/shard_map/ppermute | solution.py:44
  30.5 6.1 %collective-permute-start.8 = (f32[4,2048]{1,0:T(4,128)S(1)}, f32[4,2048]{1,0:T(4,128)S(1)}, u32[]{:S(2)}, u32[]{:S(2)}) collective-permute-start(f32[4,2048]{1,0:T(4,128)S(1)} %shard_map.51.refs_0_), channel_id=1, source_target_pairs={{0,6},{1,7},{2,4},{3,5},{4,2},{5,3},{6,0},{7,1},{8,14},{9,15},{10,... | collective-permute-start | bytes 98312 | tf_op jit(solution)/shard_map/ppermute | solution.py:44
  33.2 4.8 %collective-permute-start.7 = (f32[4,2048]{1,0:T(4,128)S(1)}, f32[4,2048]{1,0:T(4,128)S(1)}, u32[]{:S(2)}, u32[]{:S(2)}) collective-permute-start(f32[4,2048]{1,0:T(4,128)S(1)} %shard_map.51.refs_0_), channel_id=1, source_target_pairs={{0,4},{1,5},{2,6},{3,7},{4,0},{5,1},{6,2},{7,3},{8,12},{9,13},{10,... | collective-permute-start | bytes 98312 | tf_op jit(solution)/shard_map/ppermute | solution.py:44
  33.8 4.3 %collective-permute-start.6 = (f32[4,2048]{1,0:T(4,128)S(1)}, f32[4,2048]{1,0:T(4,128)S(1)}, u32[]{:S(2)}, u32[]{:S(2)}) collective-permute-start(f32[4,2048]{1,0:T(4,128)S(1)} %shard_map.51.refs_0_), channel_id=1, source_target_pairs={{0,2},{1,3},{2,0},{3,1},{4,6},{5,7},{6,4},{7,5},{8,10},{9,11},{10,... | collective-permute-start | bytes 98312 | tf_op jit(solution)/shard_map/ppermute | solution.py:44
  34.9 15.6 %collective-permute-start.4 = (f32[2,2048]{1,0:T(2,128)S(1)}, f32[2,2048]{1,0:T(2,128)S(1)}, u32[]{:S(2)}, u32[]{:S(2)}) collective-permute-start(f32[2,2048]{1,0:T(2,128)S(1)} %broadcast_select_fusion), channel_id=1, source_target_pairs={{0,1},{1,0},{2,3},{3,2},{4,5},{5,4},{6,7},{7,6},{8,9},{9,8},{10,11... | collective-permute-start | bytes 49160 | tf_op jit(solution)/shard_map/ppermute | solution.py:44
